TPU v7x, 32 devices: a whole 2x2x4 slice. The times are simulated.
32 devices in a mesh: seq: 16 (over z, y, core), tp: 2 (over x).
Axes of the slice: x: 2, y: 2, z: 4, core: 2. Of those that a mesh axis runs over, the one named last changes fastest.
Arguments:
- hidden: bfloat16 [2048, 7168], P('seq', 'tp'), may hold values from -6 to 6
- w_kv_down: bfloat16 [7168, 576], P('tp'), may hold values from -0.0625 to 0.0625
- kv_gain: float32 [512], replicated, may hold values from 0.1 to 1.9
- q_latent: bfloat16 [2048, 64, 512], P('seq', 'tp'), may hold values from -300 to 300
- q_rope: bfloat16 [2048, 4096], P('seq', 'tp'), may hold values from -6 to 6
- w_value: bfloat16 [64, 512, 128], P('tp'), may hold values from -0.75 to 0.75
Outputs:
- attended: bfloat16 [2048, 8192], P('seq', 'tp')
All inputs are finite; a program needn't handle non-finite values.
Results may differ from a plain program's by a relative error of at most 0.0097.
Values may be sent and summed in bfloat16 or wider, within the bound.
No kernel may reach another device: no remote copies, remote signals or barrier semaphores. Data moves between devices by JAX's collectives and lax.ppermute only.
A program may use at most 128 MiB of HBM per device.

v0:
```python
import functools

import jax
import jax.numpy as jnp
from jax import lax
from jax.experimental import pallas as pl
from jax.experimental.pallas import tpu as pltpu
from jax.sharding import PartitionSpec as P


KV_RANK = 512
ROPE = 64
LANES = 128
GROUP = 4

SCORE_SCALE = 192.0 ** (-0.5)
LOG2_E = 1.4426950408889634
EXP2_SCALE = SCORE_SCALE * LOG2_E
ROPE_BASE = 10000.0
EPSILON = 1e-06
MASKED = -1e30
CHUNK = 4
VMEM_LIMIT = 24 * 1024 * 1024
SMALL_VMEM = 8 * 1024 * 1024
FULL_VMEM = 60 * 1024 * 1024
PROJECT_STEPS = (896, 512, 256, 128)


def tables(positions):
    half = ROPE // 2
    frequency = ROPE_BASE ** (-jnp.arange(half, dtype=jnp.float32) * 2.0 / ROPE)
    angles = positions.astype(jnp.float32)[:, None] * frequency[None, :]
    cosine, sine = jnp.cos(angles), jnp.sin(angles)
    return jnp.concatenate([cosine, cosine], -1), jnp.concatenate([-sine, sine], -1)


def swap_halves(values):
    half = ROPE // 2
    return jnp.concatenate([values[..., half:], values[..., :half]], -1)


def project_kernel(hidden_ref, weight_ref, out_ref, hidden_vmem, weight_vmem, sems):
    depth = hidden_ref.shape[1]
    steps = sems.shape[1]
    size = depth // steps
    copies = []
    for k in range(steps):
        at = pl.ds(k * size, size)
        pair = (
            pltpu.make_async_copy(weight_ref.at[:, at], weight_vmem.at[:, at], sems.at[0, k]),
            pltpu.make_async_copy(hidden_ref.at[:, at], hidden_vmem.at[:, at], sems.at[1, k]),
        )
        for copy in pair:
            copy.start()
        copies.append(pair)
    total = None
    for k, pair in enumerate(copies):
        for copy in pair:
            copy.wait()
        at = slice(k * size, (k + 1) * size)
        part = lax.dot_general(
            hidden_vmem[:, at],
            weight_vmem[:, at],
            (((1,), (1,)), ((), ())),
            preferred_element_type=jnp.float32,
        )
        total = part if total is None else total + part
    out_ref[...] = total


def down_project(hidden, weight_t):
    rows, depth = hidden.shape
    width = weight_t.shape[0]
    size = next(s for s in PROJECT_STEPS if depth % s == 0)
    return pl.pallas_call(
        project_kernel,
        out_shape=jax.ShapeDtypeStruct((rows, width), jnp.float32),
        in_specs=[pl.BlockSpec(memory_space=pltpu.HBM)] * 2,
        out_specs=pl.BlockSpec(memory_space=pltpu.VMEM),
        scratch_shapes=[
            pltpu.VMEM(hidden.shape, hidden.dtype),
            pltpu.VMEM(weight_t.shape, weight_t.dtype),
            pltpu.SemaphoreType.DMA((2, depth // size)),
        ],
        cost_estimate=pl.CostEstimate(
            flops=2 * rows * depth * width, bytes_accessed=2 * depth * (rows + width), transcendentals=0
        ),
        compiler_params=pltpu.CompilerParams(vmem_limit_bytes=FULL_VMEM),
        name="down_project",
    )(hidden, weight_t)


def finish_kernel(own_ref, other_ref, gain_ref, cos_ref, sin_ref, ready_ref, out_ref):
    del ready_ref
    projection = own_ref[...] + other_ref[...]
    latent = projection[:, :KV_RANK]
    mean_square = jnp.mean(latent * latent, axis=-1, keepdims=True)
    normed = latent * lax.rsqrt(mean_square + EPSILON) * gain_ref[...]
    rope = projection[:, KV_RANK:]
    rotated = rope * cos_ref[...] + swap_halves(rope) * sin_ref[...]
    out_ref[:, :KV_RANK] = normed.astype(jnp.bfloat16)
    out_ref[:, KV_RANK:] = rotated.astype(jnp.bfloat16)


def finish(own, other, gain, cosine, sine, ready):
    return pl.pallas_call(
        finish_kernel,
        out_shape=jax.ShapeDtypeStruct(own.shape, jnp.bfloat16),
        in_specs=[pl.BlockSpec(memory_space=pltpu.VMEM)] * 5 + [pl.BlockSpec(memory_space=pl.ANY)],
        out_specs=pl.BlockSpec(memory_space=pltpu.VMEM),
        compiler_params=pltpu.CompilerParams(vmem_limit_bytes=SMALL_VMEM),
        name="finish_keys",
    )(own, other, gain[None, :], cosine, sine, ready)


def block_bias(index, tag, tokens, rows):
    kind, amount = tag
    if kind == "plane":
        key = (index ^ amount) * tokens + lax.broadcasted_iota(jnp.int32, (rows, tokens), 1)
        query = index * tokens + lax.broadcasted_iota(jnp.int32, (rows, tokens), 0)
        return jnp.where(key <= query, 0.0, MASKED)
    return jnp.full((rows, tokens), jnp.where(index // GROUP >= amount, 0.0, MASKED), jnp.float32)


def attend_kernel(tags, first, last, index_ref, latent_ref, rope_ref, *refs):
    key_refs, rest = refs[: len(tags)], list(refs[len(tags) :])
    heads, tokens = latent_ref.shape[:2]
    rows = heads * tokens
    index = index_ref[0]
    query = jnp.concatenate(
        [latent_ref[...].reshape(rows, KV_RANK), rope_ref[...].reshape(rows, ROPE)], -1
    )
    wide = lambda column: jnp.broadcast_to(column, (rows, LANES))
    spread = lambda value, width: jnp.concatenate([value] * (width // LANES), -1)
    top = total = mixed = None
    if not first:
        mixed, top, total = (ref[...].reshape(rows, ref.shape[2]) for ref in rest[:3])
        rest = rest[3:]
    for begin in range(0, len(tags), CHUNK):
        group = range(begin, min(begin + CHUNK, len(tags)))
        keys = jnp.concatenate([key_refs[i][...] for i in group], 0)
        count = keys.shape[0]
        scores = lax.dot_general(
            query, keys, (((1,), (1,)), ((), ())), preferred_element_type=jnp.float32
        )
        plane = tags[begin][0] == "plane"
        bias = jnp.concatenate(
            [block_bias(index, tags[i], tokens, tokens if plane else 1) for i in group], -1
        )
        if plane:
            scores = (scores.reshape(heads, tokens, count) + bias[None]).reshape(rows, count)
        else:
            scores = scores + bias
        chunk_top = wide(jnp.max(scores, axis=-1, keepdims=True))
        new_top = chunk_top if top is None else jnp.maximum(top, chunk_top)
        weights = jnp.exp2((scores - spread(new_top, count)) * EXP2_SCALE)
        chunk_total = wide(jnp.sum(weights, axis=-1, keepdims=True))
        chunk_mixed = jnp.dot(
            weights.astype(jnp.bfloat16), keys[:, :KV_RANK], preferred_element_type=jnp.float32
        )
        if top is None:
            total, mixed = chunk_total, chunk_mixed
        else:
            rescale = jnp.exp2((top - new_top) * EXP2_SCALE)
            total = total * rescale + chunk_total
            mixed = mixed * spread(rescale, KV_RANK) + chunk_mixed
        top = new_top
    if last:
        value_ref, out_ref = rest
        latent_out = (mixed / spread(total, KV_RANK)).astype(jnp.bfloat16)
        width = value_ref.shape[2]
        for h in range(heads):
            out_ref[:, h * width : (h + 1) * width] = jnp.dot(
                latent_out[h * tokens : (h + 1) * tokens],
                value_ref[h],
                preferred_element_type=jnp.float32,
            ).astype(jnp.bfloat16)
    else:
        for ref, value in zip(rest, (mixed, top, total)):
            ref[...] = value.reshape(ref.shape)


def attend(index, latent, rope, tagged, state=(), w_value=None):
    first, last = not state, w_value is not None
    tags, keys = zip(*tagged)
    all_heads, tokens, _ = latent.shape
    heads = next(h for h in (8, 4, 2, 1) if all_heads % h == 0)
    count = sum(k.shape[0] for k in keys)
    by_head = lambda a: pl.BlockSpec((heads,) + a.shape[1:], lambda g: (g, 0, 0))
    whole = lambda a: pl.BlockSpec(a.shape, lambda g: (0,) * a.ndim)
    operands = [index, latent, rope, *keys, *state]
    in_specs = [pl.BlockSpec(memory_space=pltpu.SMEM), by_head(latent), by_head(rope)]
    in_specs += [whole(k) for k in keys] + [by_head(a) for a in state]
    if last:
        width = w_value.shape[2]
        operands.append(w_value)
        in_specs.append(by_head(w_value))
        out_shape = jax.ShapeDtypeStruct((tokens, all_heads * width), jnp.bfloat16)
        out_specs = pl.BlockSpec((tokens, heads * width), lambda g: (0, g))
    else:
        out_shape = tuple(
            jax.ShapeDtypeStruct((all_heads, tokens, width), jnp.float32)
            for width in (KV_RANK, LANES, LANES)
        )
        out_specs = tuple(by_head(a) for a in out_shape)
    return pl.pallas_call(
        functools.partial(attend_kernel, tags, first, last),
        out_shape=out_shape,
        grid=(all_heads // heads,),
        in_specs=in_specs,
        out_specs=out_specs,
        input_output_aliases={} if first or last else {len(operands) - len(state) + i: i for i in range(len(state))},
        compiler_params=pltpu.CompilerParams(vmem_limit_bytes=VMEM_LIMIT),
        cost_estimate=pl.CostEstimate(
            flops=2 * all_heads * tokens * count * (2 * KV_RANK + ROPE),
            bytes_accessed=2 * all_heads * tokens * (KV_RANK + ROPE),
            transcendentals=all_heads * tokens * count,
        ),
        name="attend",
    )(*operands)


def shards(seq_size, tp_size, hidden, w_kv_down, kv_gain, q_latent, q_rope, w_value):
    tokens = hidden.shape[0]
    heads = q_latent.shape[1]
    index = lax.axis_index("seq")
    positions = index * tokens + jnp.arange(tokens, dtype=jnp.int32)
    index = index.reshape(1)

    def from_seq(value, xor):
        return lax.ppermute(value, "seq", [(i, i ^ xor) for i in range(seq_size)])

    def from_below(value, planes):
        shift = planes * GROUP
        return lax.ppermute(value, "seq", [(i, i + shift) for i in range(seq_size - shift)])

    own = down_project(hidden, w_kv_down.T)
    stride = 1
    while True:
        other = lax.ppermute(own, "tp", [(i, i ^ stride) for i in range(tp_size)])
        stride *= 2
        if stride >= tp_size:
            break
        own = own + other
    cosine, sine = tables(positions)
    latent = jnp.transpose(q_latent, (1, 0, 2))
    key_here = finish(own, other, kv_gain, cosine, sine, latent)

    rope = q_rope.astype(jnp.float32).reshape(tokens, heads, ROPE)
    rope = rope * cosine[:, None, :] + swap_halves(rope) * sine[:, None, :]
    rope = jnp.transpose(rope.astype(jnp.bfloat16), (1, 0, 2))

    levels = range(1, seq_size // GROUP)
    key_y = from_seq(key_here, 2)
    below = {d: from_below(key_here, d) for d in levels}
    plane = [key_here, key_y, from_seq(key_here, 1), from_seq(key_y, 1)]
    below_y = {d: from_seq(below[d], 2) for d in levels}
    below_core = {d: from_seq(below[d], 1) for d in levels}
    below_yc = {d: from_seq(below_y[d], 1) for d in levels}
    tag = lambda group: [(("below", d), group[d]) for d in group]

    state = attend(index, latent, rope, [(("plane", x), k) for x, k in zip((0, 2, 1, 3), plane)])
    early = tag(below) + tag({1: below_y[1]})
    late = tag({d: below_y[d] for d in levels if d > 1}) + tag(below_core) + tag(below_yc)
    state = attend(index, latent, rope, early, state=state)
    return attend(index, latent, rope, late, state=state, w_value=w_value)


def solution(mesh):
    placed = (
        P("seq", "tp"),
        P("tp", None),
        P(),
        P("seq", "tp", None),
        P("seq", "tp"),
        P("tp", None, None),
    )
    body = functools.partial(shards, mesh.shape["seq"], mesh.shape["tp"])

    return jax.shard_map(
        body, mesh=mesh, in_specs=placed, out_specs=P("seq", "tp"), check_vma=False
    )
```

profile of v0, /device:TPU:25, one launch (start us, length us, event | category | flops | bytes accessed | tf_op | source)
XLA Modules:
  0.0 71.5 jit_solution(14443732326199611114)
XLA Ops:
  0.0 4.3 %down_project.1.own_ref = f32[128,576]{1,0:T(8,128)} custom-call(bf16[128,3584]{1,0:T(8,128)(2,1)} %hidden_ref.1, bf16[576,3584]{1,0:T(8,128)(2,1)} %bitcast.15), custom_call_target="tpu_custom_call" | custom-call | flops 528482304 | bytes 5046272 | tf_op jit(solution)/shard_map/down_project/pallas_call | solution.py:75
  4.4 1.3 %collective-permute-start = (f32[128,576]{1,0:T(8,128)}, f32[128,576]{1,0:T(8,128)S(1)}, u32[]{:S(2)}, u32[]{:S(2)}) collective-permute-start(f32[128,576]{1,0:T(8,128)} %down_project.1.own_ref), channel_id=1, source_target_pairs={{0,1},{1,0},{2,3},{3,2},{4,5},{5,4},{6,7},{7,6},{8,9},{9,8},{10,11... | collective-permute-start | bytes 884744 | tf_op jit(solution)/shard_map/ppermute | solution.py:240
  5.6 0.0 copy-start.5
  5.7 6.5 %copy.23 = bf16[128,32,512]{2,0,1:T(8,128)(2,1)} copy(bf16[128,32,512]{2,1,0:T(8,128)(2,1)} %param.9) | data formatting | bytes 8388608 | tf_op args[3]
  12.2 0.0 copy-done.5
  12.2 0.0 copy-start.2
  12.2 0.0 copy-start.3
  12.2 0.3 copy.17
  12.5 0.4 copy.19
  12.9 0.3 multiply_cosine_fusion
  13.2 0.1 pad_maximum_fusion
  13.3 0.0 collective-permute-done.other_ref
  13.3 0.0 copy-done.2
  13.3 0.0 copy-done.3
  13.3 0.0 copy-start
  13.3 2.2 %copy-done = bf16[128,32,512]{2,0,1:T(8,128)(2,1)S(1)} copy-done((bf16[128,32,512]{2,0,1:T(8,128)(2,1)S(1)}, bf16[128,32,512]{2,0,1:T(8,128)(2,1)}, u32[]{:S(2)}) %copy-start) | copy-done | bytes 4194328
  15.5 0.1 finish_keys.1.refs_0_
  15.6 1.3 %collective-permute-start.13 = (bf16[128,576]{1,0:T(8,128)(2,1)S(1)}, bf16[128,576]{1,0:T(8,128)(2,1)S(1)}, u32[]{:S(2)}, u32[]{:S(2)}) collective-permute-start(bf16[128,576]{1,0:T(8,128)(2,1)S(1)} %finish_keys.1.refs_0_), channel_id=1, source_target_pairs={{0,4},{2,6},{4,0},{6,2},{8,12},{10,14},{12,8},{14,10},{16,20},{18,... | collective-permute-start | bytes 442376 | tf_op jit(solution)/shard_map/ppermute | solution.py:231
  16.9 0.7 %fusion.4 = (f32[128,32,32]{2,0,1:T(8,128)S(1)}, f32[128,32,32]{2,0,1:T(8,128)S(1)}) fusion(f32[128,32,64]{2,0,1:T(8,128)S(1)} %copy.19), kind=kLoop, calls=%fused_computation.12 | loop fusion | bytes 2097152 | tf_op jit(solution)/shard_map/slice | solution.py:39
  17.7 1.8 %collective-permute-start.14 = (bf16[128,576]{1,0:T(8,128)(2,1)S(1)}, bf16[128,576]{1,0:T(8,128)(2,1)S(1)}, u32[]{:S(2)}, u32[]{:S(2)}) collective-permute-start(bf16[128,576]{1,0:T(8,128)(2,1)S(1)} %finish_keys.1.refs_0_), channel_id=1, source_target_pairs={{0,2},{2,0},{4,6},{6,4},{8,10},{10,8},{12,14},{14,12},{16,18},{18,... | collective-permute-start | bytes 442376 | tf_op jit(solution)/shard_map/ppermute | solution.py:231
  19.5 1.3 %collective-permute-start.5 = (bf16[128,576]{1,0:T(8,128)(2,1)S(1)}, bf16[128,576]{1,0:T(8,128)(2,1)S(1)}, u32[]{:S(2)}, u32[]{:S(2)}) collective-permute-start(bf16[128,576]{1,0:T(8,128)(2,1)S(1)} %finish_keys.1.refs_0_), channel_id=1, source_target_pairs={{0,8},{2,10},{4,12},{6,14},{8,16},{10,18},{12,20},{14,22},{16,24},... | collective-permute-start | bytes 442376 | tf_op jit(solution)/shard_map/ppermute | solution.py:235
  20.8 1.3 %collective-permute-start.1 = (bf16[128,576]{1,0:T(8,128)(2,1)S(1)}, bf16[128,576]{1,0:T(8,128)(2,1)S(1)}, u32[]{:S(2)}, u32[]{:S(2)}) collective-permute-start(bf16[128,576]{1,0:T(8,128)(2,1)S(1)} %finish_keys.1.refs_0_), channel_id=1, source_target_pairs={{0,16},{2,18},{4,20},{6,22},{8,24},{10,26},{12,28},{14,30},{1,17},... | collective-permute-start | bytes 442376 | tf_op jit(solution)/shard_map/ppermute | solution.py:235
  22.1 1.5 %collective-permute-start.3 = (bf16[128,576]{1,0:T(8,128)(2,1)S(1)}, bf16[128,576]{1,0:T(8,128)(2,1)S(1)}, u32[]{:S(2)}, u32[]{:S(2)}) collective-permute-start(bf16[128,576]{1,0:T(8,128)(2,1)S(1)} %finish_keys.1.refs_0_), channel_id=1, source_target_pairs={{0,24},{2,26},{4,28},{6,30},{1,25},{3,27},{5,29},{7,31}} | collective-permute-start | bytes 442376 | tf_op jit(solution)/shard_map/ppermute | solution.py:235
  23.6 0.0 collective-permute-done.13.refs_1_
  23.6 0.1 collective-permute-start.15
  23.7 0.0 copy-start.1
  23.7 0.7 fusion.2.rope_ref
  24.4 2.9 %collective-permute-done.5.refs_0_ = bf16[128,576]{1,0:T(8,128)(2,1)S(1)} collective-permute-done((bf16[128,576]{1,0:T(8,128)(2,1)S(1)}, bf16[128,576]{1,0:T(8,128)(2,1)S(1)}, u32[]{:S(2)}, u32[]{:S(2)}) %collective-permute-start.5) | collective-permute-done | bytes 147488 | tf_op jit(solution)/shard_map/ppermute | solution.py:235
  27.2 0.2 collective-permute-start.9
  27.4 0.0 collective-permute-done.14.refs_2_
  27.4 1.8 %collective-permute-start.6 = (bf16[128,576]{1,0:T(8,128)(2,1)S(1)}, bf16[128,576]{1,0:T(8,128)(2,1)S(1)}, u32[]{:S(2)}, u32[]{:S(2)}) collective-permute-start(bf16[128,576]{1,0:T(8,128)(2,1)S(1)} %collective-permute-done.5.refs_0_), channel_id=1, source_target_pairs={{0,2},{2,0},{4,6},{6,4},{8,10},{10,8},{12,14},{14,12},{16,18},{18,... | collective-permute-start | bytes 442376 | tf_op jit(solution)/shard_map/ppermute | solution.py:231
  29.2 8.3 %collective-permute-done.1.refs_1_ = bf16[128,576]{1,0:T(8,128)(2,1)S(1)} collective-permute-done((bf16[128,576]{1,0:T(8,128)(2,1)S(1)}, bf16[128,576]{1,0:T(8,128)(2,1)S(1)}, u32[]{:S(2)}, u32[]{:S(2)}) %collective-permute-start.1) | collective-permute-done | bytes 147488 | tf_op jit(solution)/shard_map/ppermute | solution.py:235
  37.5 0.2 collective-permute-start.2
  37.8 0.0 collective-permute-done.3.refs_2_
  37.8 1.2 %collective-permute-start.7 = (bf16[128,576]{1,0:T(8,128)(2,1)S(1)}, bf16[128,576]{1,0:T(8,128)(2,1)S(1)}, u32[]{:S(2)}, u32[]{:S(2)}) collective-permute-start(bf16[128,576]{1,0:T(8,128)(2,1)S(1)} %collective-permute-done.1.refs_1_), channel_id=1, source_target_pairs={{0,2},{2,0},{4,6},{6,4},{8,10},{10,8},{12,14},{14,12},{16,18},{18,... | collective-permute-start | bytes 442376 | tf_op jit(solution)/shard_map/ppermute | solution.py:231
  38.9 0.0 collective-permute-done.15.refs_3_
  38.9 1.2 %collective-permute-start.4 = (bf16[128,576]{1,0:T(8,128)(2,1)S(1)}, bf16[128,576]{1,0:T(8,128)(2,1)S(1)}, u32[]{:S(2)}, u32[]{:S(2)}) collective-permute-start(bf16[128,576]{1,0:T(8,128)(2,1)S(1)} %collective-permute-done.3.refs_2_), channel_id=1, source_target_pairs={{0,4},{2,6},{4,0},{6,2},{8,12},{10,14},{12,8},{14,10},{16,20},{18,... | collective-permute-start | bytes 442376 | tf_op jit(solution)/shard_map/ppermute | solution.py:231
  40.2 0.0 copy-done.1
  40.2 6.7 %attend.3 = (f32[32,128,512]{2,1,0:T(8,128)S(1)}, f32[32,128,128]{2,1,0:T(8,128)S(1)}, f32[32,128,128]{2,1,0:T(8,128)S(1)}) custom-call(s32[1]{0:T(128)} %bitcast.index_ref, bf16[32,128,512]{2,1,0:T(8,128)(2,1)S(1)} %bitcast.11, bf16[32,128,64]{2,1,0:T(8,128)(2,1)S(1)} %fusion.2.rope_ref, bf16[128,576]{1,0:T(8,128)(2,1)S(1)} %finish_keys.1.refs_0_, ...), custom_call_target="tpu_custom_call" | custom-call | flops 4563402752 | bytes 4718592 | tf_op jit(solution)/shard_map/attend/pallas_call | solution.py:206
  46.9 0.0 collective-permute-done.9.refs_3_
  46.9 0.4 collective-permute-start.8
  47.3 0.0 collective-permute-done.2.refs_0_
  47.3 0.2 collective-permute-start.10
  47.5 0.0 collective-permute-done.4.refs_1_
  47.5 0.4 collective-permute-start.11
  47.8 0.0 collective-permute-done.6.refs_2_
  47.8 0.2 collective-permute-start.12
  48.0 0.0 copy-start.4
  48.0 8.1 %attend.4 = (f32[32,128,512]{2,1,0:T(8,128)S(1)}, f32[32,128,128]{2,1,0:T(8,128)S(1)}, f32[32,128,128]{2,1,0:T(8,128)S(1)}) custom-call(s32[1]{0:T(128)} %bitcast.index_ref, bf16[32,128,512]{2,1,0:T(8,128)(2,1)S(1)} %bitcast.12, bf16[32,128,64]{2,1,0:T(8,128)(2,1)S(1)} %fusion.2.rope_ref, ...), custom_call_target="tpu_custom_call", output_to_operand_aliasing={{0}: (7, {}), {1}: (8, {}), {2}: (9, {})} | custom-call | flops 4563402752 | bytes 4718592 | tf_op jit(solution)/shard_map/attend/pallas_call | solution.py:206
  56.1 0.0 collective-permute-done.7.refs_3_
  56.1 0.0 collective-permute-done.8.refs_4_
  56.1 0.0 collective-permute-done.10.refs_5_
  56.1 0.0 collective-permute-done.11.refs_6_
  56.1 0.0 collective-permute-done.12.refs_7_
  56.2 0.0 copy-done.4
  56.2 15.4 %attend.5 = bf16[128,4096]{1,0:T(8,128)(2,1)} custom-call(s32[1]{0:T(128)} %bitcast.index_ref, bf16[32,128,512]{2,1,0:T(8,128)(2,1)S(1)} %bitcast.13, bf16[32,128,64]{2,1,0:T(8,128)(2,1)S(1)} %fusion.2.rope_ref, bf16[128,576]{1,0:T(8,128)(2,1)S(1)} %collective-permute-done.2.refs_0_, bf16[128,576]{1,0:T(8,128)(2,1)S(1)} %collective-permute-done.4.refs_1_, ...), custom_call_target="tpu_custom_call" | custom-call | flops 9126805504 | bytes 4718592 | tf_op jit(solution)/shard_map/attend/pallas_call | solution.py:206
  (2 shorter events, 0.0 us)
Async XLA Ops:
  4.4 8.9 %collective-permute-start = (f32[128,576]{1,0:T(8,128)}, f32[128,576]{1,0:T(8,128)S(1)}, u32[]{:S(2)}, u32[]{:S(2)}) collective-permute-start(f32[128,576]{1,0:T(8,128)} %down_project.1.own_ref), channel_id=1, source_target_pairs={{0,1},{1,0},{2,3},{3,2},{4,5},{5,4},{6,7},{7,6},{8,9},{9,8},{10,11... | collective-permute-start | bytes 884744 | tf_op jit(solution)/shard_map/ppermute | solution.py:240
  5.6 6.5 %copy-start.5 = (bf16[128,2048]{1,0:T(8,128)(2,1)S(1)}, bf16[128,2048]{1,0:T(8,128)(2,1)}, u32[]{:S(2)}) copy-start(bf16[128,2048]{1,0:T(8,128)(2,1)} %param.10) | copy-start | bytes 1572868
  12.2 1.1 %copy-start.2 = (f32[128,576]{1,0:T(8,128)S(1)}, f32[128,576]{1,0:T(8,128)}, u32[]{:S(2)}) copy-start(f32[128,576]{1,0:T(8,128)} %down_project.1.own_ref) | copy-start | bytes 884740
  12.2 1.1 %copy-start.3 = (f32[512]{0:T(512)S(1)}, f32[512]{0:T(512)}, u32[]{:S(2)}) copy-start(f32[512]{0:T(512)} %param.8) | copy-start | bytes 6148
  13.3 2.2 %copy-start = (bf16[128,32,512]{2,0,1:T(8,128)(2,1)S(1)}, bf16[128,32,512]{2,0,1:T(8,128)(2,1)}, u32[]{:S(2)}) copy-start(bf16[128,32,512]{2,0,1:T(8,128)(2,1)} %copy.23) | copy-start | bytes 12582916
  15.6 7.9 %collective-permute-start.13 = (bf16[128,576]{1,0:T(8,128)(2,1)S(1)}, bf16[128,576]{1,0:T(8,128)(2,1)S(1)}, u32[]{:S(2)}, u32[]{:S(2)}) collective-permute-start(bf16[128,576]{1,0:T(8,128)(2,1)S(1)} %finish_keys.1.refs_0_), channel_id=1, source_target_pairs={{0,4},{2,6},{4,0},{6,2},{8,12},{10,14},{12,8},{14,10},{16,20},{18,... | collective-permute-start | bytes 442376 | tf_op jit(solution)/shard_map/ppermute | solution.py:231
  17.7 9.7 %collective-permute-start.14 = (bf16[128,576]{1,0:T(8,128)(2,1)S(1)}, bf16[128,576]{1,0:T(8,128)(2,1)S(1)}, u32[]{:S(2)}, u32[]{:S(2)}) collective-permute-start(bf16[128,576]{1,0:T(8,128)(2,1)S(1)} %finish_keys.1.refs_0_), channel_id=1, source_target_pairs={{0,2},{2,0},{4,6},{6,4},{8,10},{10,8},{12,14},{14,12},{16,18},{18,... | collective-permute-start | bytes 442376 | tf_op jit(solution)/shard_map/ppermute | solution.py:231
  19.5 7.7 %collective-permute-start.5 = (bf16[128,576]{1,0:T(8,128)(2,1)S(1)}, bf16[128,576]{1,0:T(8,128)(2,1)S(1)}, u32[]{:S(2)}, u32[]{:S(2)}) collective-permute-start(bf16[128,576]{1,0:T(8,128)(2,1)S(1)} %finish_keys.1.refs_0_), channel_id=1, source_target_pairs={{0,8},{2,10},{4,12},{6,14},{8,16},{10,18},{12,20},{14,22},{16,24},... | collective-permute-start | bytes 442376 | tf_op jit(solution)/shard_map/ppermute | solution.py:235
  20.8 16.7 %collective-permute-start.1 = (bf16[128,576]{1,0:T(8,128)(2,1)S(1)}, bf16[128,576]{1,0:T(8,128)(2,1)S(1)}, u32[]{:S(2)}, u32[]{:S(2)}) collective-permute-start(bf16[128,576]{1,0:T(8,128)(2,1)S(1)} %finish_keys.1.refs_0_), channel_id=1, source_target_pairs={{0,16},{2,18},{4,20},{6,22},{8,24},{10,26},{12,28},{14,30},{1,17},... | collective-permute-start | bytes 442376 | tf_op jit(solution)/shard_map/ppermute | solution.py:235
  22.1 15.7 %collective-permute-start.3 = (bf16[128,576]{1,0:T(8,128)(2,1)S(1)}, bf16[128,576]{1,0:T(8,128)(2,1)S(1)}, u32[]{:S(2)}, u32[]{:S(2)}) collective-permute-start(bf16[128,576]{1,0:T(8,128)(2,1)S(1)} %finish_keys.1.refs_0_), channel_id=1, source_target_pairs={{0,24},{2,26},{4,28},{6,30},{1,25},{3,27},{5,29},{7,31}} | collective-permute-start | bytes 442376 | tf_op jit(solution)/shard_map/ppermute | solution.py:235
  23.6 15.4 %collective-permute-start.15 = (bf16[128,576]{1,0:T(8,128)(2,1)S(1)}, bf16[128,576]{1,0:T(8,128)(2,1)S(1)}, u32[]{:S(2)}, u32[]{:S(2)}) collective-permute-start(bf16[128,576]{1,0:T(8,128)(2,1)S(1)} %collective-permute-done.13.refs_1_), channel_id=1, source_target_pairs={{0,2},{2,0},{4,6},{6,4},{8,10},{10,8},{12,14},{14,12},{16,18},{18,... | collective-permute-start | bytes 442376 | tf_op jit(solution)/shard_map/ppermute | solution.py:231
  23.7 16.5 %copy-start.1 = (bf16[128,32,512]{2,0,1:T(8,128)(2,1)S(1)}, bf16[128,32,512]{2,0,1:T(8,128)(2,1)}, u32[]{:S(2)}) copy-start(bf16[128,32,512]{2,0,1:T(8,128)(2,1)} %copy.23) | copy-start | bytes 12582916
  27.2 19.7 %collective-permute-start.9 = (bf16[128,576]{1,0:T(8,128)(2,1)S(1)}, bf16[128,576]{1,0:T(8,128)(2,1)S(1)}, u32[]{:S(2)}, u32[]{:S(2)}) collective-permute-start(bf16[128,576]{1,0:T(8,128)(2,1)S(1)} %collective-permute-done.5.refs_0_), channel_id=1, source_target_pairs={{0,4},{2,6},{4,0},{6,2},{8,12},{10,14},{12,8},{14,10},{16,20},{18,... | collective-permute-start | bytes 442376 | tf_op jit(solution)/shard_map/ppermute | solution.py:231
  27.4 20.4 %collective-permute-start.6 = (bf16[128,576]{1,0:T(8,128)(2,1)S(1)}, bf16[128,576]{1,0:T(8,128)(2,1)S(1)}, u32[]{:S(2)}, u32[]{:S(2)}) collective-permute-start(bf16[128,576]{1,0:T(8,128)(2,1)S(1)} %collective-permute-done.5.refs_0_), channel_id=1, source_target_pairs={{0,2},{2,0},{4,6},{6,4},{8,10},{10,8},{12,14},{14,12},{16,18},{18,... | collective-permute-start | bytes 442376 | tf_op jit(solution)/shard_map/ppermute | solution.py:231
  37.5 9.8 %collective-permute-start.2 = (bf16[128,576]{1,0:T(8,128)(2,1)S(1)}, bf16[128,576]{1,0:T(8,128)(2,1)S(1)}, u32[]{:S(2)}, u32[]{:S(2)}) collective-permute-start(bf16[128,576]{1,0:T(8,128)(2,1)S(1)} %collective-permute-done.1.refs_1_), channel_id=1, source_target_pairs={{0,4},{2,6},{4,0},{6,2},{8,12},{10,14},{12,8},{14,10},{16,20},{18,... | collective-permute-start | bytes 442376 | tf_op jit(solution)/shard_map/ppermute | solution.py:231
  37.8 18.3 %collective-permute-start.7 = (bf16[128,576]{1,0:T(8,128)(2,1)S(1)}, bf16[128,576]{1,0:T(8,128)(2,1)S(1)}, u32[]{:S(2)}, u32[]{:S(2)}) collective-permute-start(bf16[128,576]{1,0:T(8,128)(2,1)S(1)} %collective-permute-done.1.refs_1_), channel_id=1, source_target_pairs={{0,2},{2,0},{4,6},{6,4},{8,10},{10,8},{12,14},{14,12},{16,18},{18,... | collective-permute-start | bytes 442376 | tf_op jit(solution)/shard_map/ppermute | solution.py:231
  38.9 8.6 %collective-permute-start.4 = (bf16[128,576]{1,0:T(8,128)(2,1)S(1)}, bf16[128,576]{1,0:T(8,128)(2,1)S(1)}, u32[]{:S(2)}, u32[]{:S(2)}) collective-permute-start(bf16[128,576]{1,0:T(8,128)(2,1)S(1)} %collective-permute-done.3.refs_2_), channel_id=1, source_target_pairs={{0,4},{2,6},{4,0},{6,2},{8,12},{10,14},{12,8},{14,10},{16,20},{18,... | collective-permute-start | bytes 442376 | tf_op jit(solution)/shard_map/ppermute | solution.py:231
  46.9 9.2 %collective-permute-start.8 = (bf16[128,576]{1,0:T(8,128)(2,1)S(1)}, bf16[128,576]{1,0:T(8,128)(2,1)S(1)}, u32[]{:S(2)}, u32[]{:S(2)}) collective-permute-start(bf16[128,576]{1,0:T(8,128)(2,1)S(1)} %collective-permute-done.3.refs_2_), channel_id=1, source_target_pairs={{0,2},{2,0},{4,6},{6,4},{8,10},{10,8},{12,14},{14,12},{16,18},{18,... | collective-permute-start | bytes 442376 | tf_op jit(solution)/shard_map/ppermute | solution.py:231
  47.3 8.8 %collective-permute-start.10 = (bf16[128,576]{1,0:T(8,128)(2,1)S(1)}, bf16[128,576]{1,0:T(8,128)(2,1)S(1)}, u32[]{:S(2)}, u32[]{:S(2)}) collective-permute-start(bf16[128,576]{1,0:T(8,128)(2,1)S(1)} %collective-permute-done.9.refs_3_), channel_id=1, source_target_pairs={{0,2},{2,0},{4,6},{6,4},{8,10},{10,8},{12,14},{14,12},{16,18},{18,... | collective-permute-start | bytes 442376 | tf_op jit(solution)/shard_map/ppermute | solution.py:231
  47.5 8.7 %collective-permute-start.11 = (bf16[128,576]{1,0:T(8,128)(2,1)S(1)}, bf16[128,576]{1,0:T(8,128)(2,1)S(1)}, u32[]{:S(2)}, u32[]{:S(2)}) collective-permute-start(bf16[128,576]{1,0:T(8,128)(2,1)S(1)} %collective-permute-done.2.refs_0_), channel_id=1, source_target_pairs={{0,2},{2,0},{4,6},{6,4},{8,10},{10,8},{12,14},{14,12},{16,18},{18,... | collective-permute-start | bytes 442376 | tf_op jit(solution)/shard_map/ppermute | solution.py:231
  47.8 8.3 %collective-permute-start.12 = (bf16[128,576]{1,0:T(8,128)(2,1)S(1)}, bf16[128,576]{1,0:T(8,128)(2,1)S(1)}, u32[]{:S(2)}, u32[]{:S(2)}) collective-permute-start(bf16[128,576]{1,0:T(8,128)(2,1)S(1)} %collective-permute-done.4.refs_1_), channel_id=1, source_target_pairs={{0,2},{2,0},{4,6},{6,4},{8,10},{10,8},{12,14},{14,12},{16,18},{18,... | collective-permute-start | bytes 442376 | tf_op jit(solution)/shard_map/ppermute | solution.py:231
  48.0 8.2 %copy-start.4 = (bf16[32,512,128]{2,1,0:T(8,128)(2,1)S(1)}, bf16[32,512,128]{2,1,0:T(8,128)(2,1)}, u32[]{:S(2)}) copy-start(bf16[32,512,128]{2,1,0:T(8,128)(2,1)} %refs_11_.1) | copy-start | bytes 12582916
where the time goes:
time: 71.7 us; the launch traced here: 71.5 us
  Pallas kernels  34.6 us (48%)
  starting transfers between devices  14.2 us (20%)
  waiting for transfers between devices  11.2 us (16%)
  local copies, waits for them, and re-layouts  10.1 us (14%)
  other arithmetic  1.1 us (2%)
    pallas_call x3, Pallas kernels, attend(): pl.pallas_call(functools.partial(attend_kernel, tags, first, last), out_s...  30.2 us
    ppermute x3, waiting for transfers between devices, from_below(): lax.ppermute(value, 'seq', [(i, i + shift) for i in range(seq_size - shif...  11.2 us
    unnamed x14, local copies, waits for them, and re-layouts  9.01 us
    ppermute x12, starting transfers between devices, from_seq(): return lax.ppermute(value, 'seq', [(i, i ^ xor) for i in range(seq_size)])  8.89 us
    pallas_call x1, Pallas kernels, down_project(): pl.pallas_call(project_kernel, out_shape=jax.ShapeDtypeStruct((rows, widt...  4.34 us
    ppermute x3, starting transfers between devices, from_below(): lax.ppermute(value, 'seq', [(i, i + shift) for i in range(seq_size - shif...  4.04 us
  transfers between devices with their start and end apart: 16, of which 2 were waited for; matrix products, arithmetic and copies ran while one was open for 13% of the time, Pallas kernels for 21%

commit v1 on v0

--- a/solution.py
+++ b/solution.py
@@ -29,14 +29,16 @@
 def tables(positions):
     half = ROPE // 2
     frequency = ROPE_BASE ** (-jnp.arange(half, dtype=jnp.float32) * 2.0 / ROPE)
+    angles = frequency[:, None] * positions.astype(jnp.float32)[None, :]
+    return jnp.cos(angles), jnp.sin(angles)
+
+
+def query_tables(positions):
+    half = ROPE // 2
+    frequency = ROPE_BASE ** (-jnp.arange(half, dtype=jnp.float32) * 2.0 / ROPE)
     angles = positions.astype(jnp.float32)[:, None] * frequency[None, :]
     cosine, sine = jnp.cos(angles), jnp.sin(angles)
-    return jnp.concatenate([cosine, cosine], -1), jnp.concatenate([-sine, sine], -1)
-
-
-def swap_halves(values):
-    half = ROPE // 2
-    return jnp.concatenate([values[..., half:], values[..., :half]], -1)
+    return jnp.concatenate([cosine] * 4, -1), jnp.concatenate([-sine, sine] * 2, -1)
 
 
 def project_kernel(hidden_ref, weight_ref, out_ref, hidden_vmem, weight_vmem, sems):
@@ -59,8 +61,8 @@
             copy.wait()
         at = slice(k * size, (k + 1) * size)
         part = lax.dot_general(
+            weight_vmem[:, at],
             hidden_vmem[:, at],
-            weight_vmem[:, at],
             (((1,), (1,)), ((), ())),
             preferred_element_type=jnp.float32,
         )
@@ -74,7 +76,7 @@
     size = next(s for s in PROJECT_STEPS if depth % s == 0)
     return pl.pallas_call(
         project_kernel,
-        out_shape=jax.ShapeDtypeStruct((rows, width), jnp.float32),
+        out_shape=jax.ShapeDtypeStruct((width, rows), jnp.float32),
         in_specs=[pl.BlockSpec(memory_space=pltpu.HBM)] * 2,
         out_specs=pl.BlockSpec(memory_space=pltpu.VMEM),
         scratch_shapes=[
@@ -90,27 +92,49 @@
     )(hidden, weight_t)
 
 
-def finish_kernel(own_ref, other_ref, gain_ref, cos_ref, sin_ref, ready_ref, out_ref):
-    del ready_ref
+def finish_kernel(own_ref, other_ref, gain_ref, cos_ref, sin_ref, latent_ref, rope_ref, out_ref):
+    del latent_ref, rope_ref
     projection = own_ref[...] + other_ref[...]
-    latent = projection[:, :KV_RANK]
-    mean_square = jnp.mean(latent * latent, axis=-1, keepdims=True)
+    latent = projection[:KV_RANK]
+    mean_square = jnp.mean(latent * latent, axis=0, keepdims=True)
     normed = latent * lax.rsqrt(mean_square + EPSILON) * gain_ref[...]
-    rope = projection[:, KV_RANK:]
-    rotated = rope * cos_ref[...] + swap_halves(rope) * sin_ref[...]
-    out_ref[:, :KV_RANK] = normed.astype(jnp.bfloat16)
-    out_ref[:, KV_RANK:] = rotated.astype(jnp.bfloat16)
-
-
-def finish(own, other, gain, cosine, sine, ready):
+    half = ROPE // 2
+    first, second = projection[KV_RANK : KV_RANK + half], projection[KV_RANK + half :]
+    cosine, sine = cos_ref[...], sin_ref[...]
+    keys = [normed, first * cosine - second * sine, first * sine + second * cosine]
+    out_ref[...] = jnp.concatenate(keys, 0).astype(jnp.bfloat16)
+
+
+def finish(own, other, gain, cosine, sine, latent, rope):
     return pl.pallas_call(
         finish_kernel,
         out_shape=jax.ShapeDtypeStruct(own.shape, jnp.bfloat16),
-        in_specs=[pl.BlockSpec(memory_space=pltpu.VMEM)] * 5 + [pl.BlockSpec(memory_space=pl.ANY)],
+        in_specs=[pl.BlockSpec(memory_space=pltpu.VMEM)] * 5 + [pl.BlockSpec(memory_space=pl.ANY)] * 2,
         out_specs=pl.BlockSpec(memory_space=pltpu.VMEM),
         compiler_params=pltpu.CompilerParams(vmem_limit_bytes=SMALL_VMEM),
         name="finish_keys",
-    )(own, other, gain[None, :], cosine, sine, ready)
+    )(own, other, gain, cosine, sine, latent, rope)
+
+
+def rotate_kernel(query_ref, cos_ref, sin_ref, out_ref):
+    cosine, sine = cos_ref[...], sin_ref[...]
+    half = ROPE // 2
+    lower = lax.broadcasted_iota(jnp.int32, cosine.shape, 1) % ROPE < half
+    for pair in range(query_ref.shape[1] // (2 * ROPE)):
+        value = query_ref[:, pair * 2 * ROPE : (pair + 1) * 2 * ROPE].astype(jnp.float32)
+        up, down = pltpu.roll(value, 2 * ROPE - half, 1), pltpu.roll(value, half, 1)
+        rotated = value * cosine + jnp.where(lower, up, down) * sine
+        out_ref[2 * pair] = rotated[:, :ROPE].astype(jnp.bfloat16)
+        out_ref[2 * pair + 1] = rotated[:, ROPE:].astype(jnp.bfloat16)
+
+
+def rotate(query, cosine, sine, heads):
+    return pl.pallas_call(
+        rotate_kernel,
+        out_shape=jax.ShapeDtypeStruct((heads, query.shape[0], ROPE), jnp.bfloat16),
+        compiler_params=pltpu.CompilerParams(vmem_limit_bytes=SMALL_VMEM),
+        name="rotate_queries",
+    )(query, cosine, sine)
 
 
 def block_bias(index, tag, tokens, rows):
@@ -127,57 +151,74 @@
     heads, tokens = latent_ref.shape[:2]
     rows = heads * tokens
     index = index_ref[0]
-    query = jnp.concatenate(
-        [latent_ref[...].reshape(rows, KV_RANK), rope_ref[...].reshape(rows, ROPE)], -1
-    )
+    state_refs = [] if first else rest[:3]
+    rest = rest[len(state_refs) :]
+    groups = [range(b, min(b + CHUNK, len(tags))) for b in range(0, len(tags), CHUNK)]
     wide = lambda column: jnp.broadcast_to(column, (rows, LANES))
     spread = lambda value, width: jnp.concatenate([value] * (width // LANES), -1)
-    top = total = mixed = None
-    if not first:
-        mixed, top, total = (ref[...].reshape(rows, ref.shape[2]) for ref in rest[:3])
-        rest = rest[3:]
-    for begin in range(0, len(tags), CHUNK):
-        group = range(begin, min(begin + CHUNK, len(tags)))
-        keys = jnp.concatenate([key_refs[i][...] for i in group], 0)
-        count = keys.shape[0]
-        scores = lax.dot_general(
-            query, keys, (((1,), (1,)), ((), ())), preferred_element_type=jnp.float32
-        )
-        plane = tags[begin][0] == "plane"
-        bias = jnp.concatenate(
-            [block_bias(index, tags[i], tokens, tokens if plane else 1) for i in group], -1
-        )
-        if plane:
-            scores = (scores.reshape(heads, tokens, count) + bias[None]).reshape(rows, count)
+
+    def run(groups):
+        top = total = mixed = None
+        if not first:
+            mixed, top, total = (ref[...].reshape(rows, ref.shape[2]) for ref in state_refs)
+        if groups:
+            query = jnp.concatenate(
+                [latent_ref[...].reshape(rows, KV_RANK), rope_ref[...].reshape(rows, ROPE)], -1
+            )
+        for group in groups:
+            keys = jnp.concatenate([key_refs[i][...] for i in group], 1)
+            count = keys.shape[1]
+            scores = jnp.dot(query, keys, preferred_element_type=jnp.float32)
+            plane = tags[group[0]][0] == "plane"
+            bias = jnp.concatenate(
+                [block_bias(index, tags[i], tokens, tokens if plane else 1) for i in group], -1
+            )
+            if plane:
+                scores = (scores.reshape(heads, tokens, count) + bias[None]).reshape(rows, count)
+            else:
+                scores = scores + bias
+            chunk_top = wide(jnp.max(scores, axis=-1, keepdims=True))
+            new_top = chunk_top if top is None else jnp.maximum(top, chunk_top)
+            weights = jnp.exp2((scores - spread(new_top, count)) * EXP2_SCALE)
+            chunk_total = wide(jnp.sum(weights, axis=-1, keepdims=True))
+            chunk_mixed = lax.dot_general(
+                weights.astype(jnp.bfloat16),
+                keys[:KV_RANK],
+                (((1,), (1,)), ((), ())),
+                preferred_element_type=jnp.float32,
+            )
+            if top is None:
+                total, mixed = chunk_total, chunk_mixed
+            else:
+                rescale = jnp.exp2((top - new_top) * EXP2_SCALE)
+                total = total * rescale + chunk_total
+                mixed = mixed * spread(rescale, KV_RANK) + chunk_mixed
+            top = new_top
+        if last:
+            value_ref, out_ref = rest
+            latent_out = (mixed / spread(total, KV_RANK)).astype(jnp.bfloat16)
+            width = value_ref.shape[2]
+            for h in range(heads):
+                out_ref[:, h * width : (h + 1) * width] = jnp.dot(
+                    latent_out[h * tokens : (h + 1) * tokens],
+                    value_ref[h],
+                    preferred_element_type=jnp.float32,
+                ).astype(jnp.bfloat16)
         else:
-            scores = scores + bias
-        chunk_top = wide(jnp.max(scores, axis=-1, keepdims=True))
-        new_top = chunk_top if top is None else jnp.maximum(top, chunk_top)
-        weights = jnp.exp2((scores - spread(new_top, count)) * EXP2_SCALE)
-        chunk_total = wide(jnp.sum(weights, axis=-1, keepdims=True))
-        chunk_mixed = jnp.dot(
-            weights.astype(jnp.bfloat16), keys[:, :KV_RANK], preferred_element_type=jnp.float32
-        )
-        if top is None:
-            total, mixed = chunk_total, chunk_mixed
-        else:
-            rescale = jnp.exp2((top - new_top) * EXP2_SCALE)
-            total = total * rescale + chunk_total
-            mixed = mixed * spread(rescale, KV_RANK) + chunk_mixed
-        top = new_top
-    if last:
-        value_ref, out_ref = rest
-        latent_out = (mixed / spread(total, KV_RANK)).astype(jnp.bfloat16)
-        width = value_ref.shape[2]
-        for h in range(heads):
-            out_ref[:, h * width : (h + 1) * width] = jnp.dot(
-                latent_out[h * tokens : (h + 1) * tokens],
-                value_ref[h],
-                preferred_element_type=jnp.float32,
-            ).astype(jnp.bfloat16)
-    else:
-        for ref, value in zip(rest, (mixed, top, total)):
-            ref[...] = value.reshape(ref.shape)
+            for ref, value in zip(rest, (mixed, top, total)):
+                ref[...] = value.reshape(ref.shape)
+
+    if first:
+        run(groups)
+        return
+    lowest = [min(tags[i][1] for i in group) for group in groups]
+    needed = sum((index // GROUP >= level).astype(jnp.int32) for level in lowest)
+    cases = sorted({0, 1, len(groups)})
+    for below, case in zip([-1] + cases, cases):
+
+        @pl.when((needed > below) & (needed <= case))
+        def _():
+            run(groups[:case])
 
 
 def attend(index, latent, rope, tagged, state=(), w_value=None):
@@ -185,7 +226,7 @@
     tags, keys = zip(*tagged)
     all_heads, tokens, _ = latent.shape
     heads = next(h for h in (8, 4, 2, 1) if all_heads % h == 0)
-    count = sum(k.shape[0] for k in keys)
+    count = sum(k.shape[1] for k in keys)
     by_head = lambda a: pl.BlockSpec((heads,) + a.shape[1:], lambda g: (g, 0, 0))
     whole = lambda a: pl.BlockSpec(a.shape, lambda g: (0,) * a.ndim)
     operands = [index, latent, rope, *keys, *state]
@@ -243,16 +284,17 @@
             break
         own = own + other
     cosine, sine = tables(positions)
-    latent = jnp.transpose(q_latent, (1, 0, 2))
-    key_here = finish(own, other, kv_gain, cosine, sine, latent)
-
-    rope = q_rope.astype(jnp.float32).reshape(tokens, heads, ROPE)
-    rope = rope * cosine[:, None, :] + swap_halves(rope) * sine[:, None, :]
-    rope = jnp.transpose(rope.astype(jnp.bfloat16), (1, 0, 2))
+    latent = lax.optimization_barrier(jnp.transpose(q_latent, (1, 0, 2)))
+    gain = jnp.broadcast_to(kv_gain[:, None], (KV_RANK, tokens))
+    rope = rotate(q_rope, *query_tables(positions), heads)
+    key_here = finish(own, other, gain, cosine, sine, latent[:1, :16, :LANES], rope)
 
     levels = range(1, seq_size // GROUP)
     key_y = from_seq(key_here, 2)
-    below = {d: from_below(key_here, d) for d in levels}
+    below = {d: from_below(key_here, d) for d in levels if d != 2}
+    if 2 in levels:
+        below[2] = from_below(below[1], 1)
+    below = {d: below[d] for d in levels}
     plane = [key_here, key_y, from_seq(key_here, 1), from_seq(key_y, 1)]
     below_y = {d: from_seq(below[d], 2) for d in levels}
     below_core = {d: from_seq(below[d], 1) for d in levels}
@@ -262,6 +304,7 @@
     state = attend(index, latent, rope, [(("plane", x), k) for x, k in zip((0, 2, 1, 3), plane)])
     early = tag(below) + tag({1: below_y[1]})
     late = tag({d: below_y[d] for d in levels if d > 1}) + tag(below_core) + tag(below_yc)
+    early, late = (sorted(group, key=lambda item: item[0][1]) for group in (early, late))
     state = attend(index, latent, rope, early, state=state)
     return attend(index, latent, rope, late, state=state, w_value=w_value)
 

time: 71.7 us -> 62.8 us (0.88)
  the two profiles are of different devices: /device:TPU:25 before, /device:TPU:19 now
where the time goes in v1:
time: 62.8 us; the launch traced here: 62.6 us
  Pallas kernels  36.8 us (59%)
  starting transfers between devices  18.9 us (30%)
  local copies, waits for them, and re-layouts  4.75 us (8%)
  waiting for transfers between devices  1.35 us (2%)
  other arithmetic  0.63 us (1%)
    pallas_call x3, Pallas kernels, attend(): pl.pallas_call(functools.partial(attend_kernel, tags, first, last), out_s...  30.9 us
    ppermute x12, starting transfers between devices, from_seq(): return lax.ppermute(value, 'seq', [(i, i ^ xor) for i in range(seq_size)])  11.6 us
    ppermute x3, starting transfers between devices, from_below(): lax.ppermute(value, 'seq', [(i, i + shift) for i in range(seq_size - shif...  6.97 us
    unnamed x9, local copies, waits for them, and re-layouts  4.62 us
    pallas_call x1, Pallas kernels, down_project(): pl.pallas_call(project_kernel, out_shape=jax.ShapeDtypeStruct((width, row...  4.33 us
    pallas_call x1, Pallas kernels, rotate(): pl.pallas_call(rotate_kernel, out_shape=jax.ShapeDtypeStruct((heads, quer...  1.48 us
  transfers between devices with their start and end apart: 16, of which 2 were waited for; matrix products, arithmetic and copies ran while one was open for 8% of the time, Pallas kernels for 26%

profile of v1, /device:TPU:19, one launch (start us, length us, event | category | flops | bytes accessed | tf_op | source)
XLA Modules:
  0.0 62.6 jit_solution(7938491612481359486)
XLA Ops:
  0.0 4.3 %down_project.1.own_ref = f32[576,128]{1,0:T(8,128)} custom-call(bf16[128,3584]{1,0:T(8,128)(2,1)} %hidden_ref.1, bf16[576,3584]{1,0:T(8,128)(2,1)} %bitcast.9), custom_call_target="tpu_custom_call" | custom-call | flops 528482304 | bytes 5046272 | tf_op jit(solution)/shard_map/down_project/pallas_call | solution.py:77
  4.3 0.3 collective-permute-start
  4.7 0.0 copy-start.1
  4.7 0.0 copy-start.3
  4.7 0.0 copy-start
  4.7 4.6 %copy.14 = bf16[128,32,512]{2,0,1:T(8,128)(2,1)S(1)} copy(bf16[128,32,512]{2,1,0:T(8,128)(2,1)} %param.9) | data formatting | bytes 8388608 | tf_op args[3]
  9.3 0.3 fusion
  9.6 0.2 pad_maximum_fusion
  9.8 0.0 copy-done.1
  9.8 1.5 %rotate_queries.1.rope_ref = bf16[32,128,64]{2,1,0:T(8,128)(2,1)S(1)} custom-call(bf16[128,2048]{1,0:T(8,128)(2,1)S(1)} %copy-done.1, f32[128,128]{1,0:T(8,128)S(1)} %get-tuple-element.22.cos_ref, f32[128,128]{1,0:T(8,128)S(1)} %get-tuple-element.23.sin_ref), custom_call_target="tpu_custom_call" | custom-call | tf_op jit(solution)/shard_map/rotate_queries/pallas_call | solution.py:132
  11.3 0.1 multiply_sine_fusion.1
  11.4 1.1 %collective-permute-done.other_ref = f32[576,128]{1,0:T(8,128)S(1)} collective-permute-done((f32[576,128]{1,0:T(8,128)}, f32[576,128]{1,0:T(8,128)S(1)}, u32[]{:S(2)}, u32[]{:S(2)}) %collective-permute-start) | collective-permute-done | bytes 294944 | tf_op jit(solution)/shard_map/ppermute | solution.py:281
  12.5 0.0 copy-done.3
  12.5 0.1 broadcast_in_dim.2.gain_ref
  12.6 0.0 copy-done
  12.7 0.1 finish_keys.1.refs_0_
  12.8 1.3 %collective-permute-start.13 = (bf16[576,128]{1,0:T(8,128)(2,1)S(1)}, bf16[576,128]{1,0:T(8,128)(2,1)S(1)}, u32[]{:S(2)}, u32[]{:S(2)}) collective-permute-start(bf16[576,128]{1,0:T(8,128)(2,1)S(1)} %finish_keys.1.refs_0_), channel_id=1, source_target_pairs={{0,4},{2,6},{4,0},{6,2},{8,12},{10,14},{12,8},{14,10},{16,20},{18,... | collective-permute-start | bytes 442376 | tf_op jit(solution)/shard_map/ppermute | solution.py:272
  14.1 3.2 %collective-permute-start.1 = (bf16[576,128]{1,0:T(8,128)(2,1)S(1)}, bf16[576,128]{1,0:T(8,128)(2,1)S(1)}, u32[]{:S(2)}, u32[]{:S(2)}) collective-permute-start(bf16[576,128]{1,0:T(8,128)(2,1)S(1)} %finish_keys.1.refs_0_), channel_id=1, source_target_pairs={{0,8},{2,10},{4,12},{6,14},{8,16},{10,18},{12,20},{14,22},{16,24},... | collective-permute-start | bytes 442376 | tf_op jit(solution)/shard_map/ppermute | solution.py:276
  17.3 2.2 %collective-permute-start.14 = (bf16[576,128]{1,0:T(8,128)(2,1)S(1)}, bf16[576,128]{1,0:T(8,128)(2,1)S(1)}, u32[]{:S(2)}, u32[]{:S(2)}) collective-permute-start(bf16[576,128]{1,0:T(8,128)(2,1)S(1)} %finish_keys.1.refs_0_), channel_id=1, source_target_pairs={{0,2},{2,0},{4,6},{6,4},{8,10},{10,8},{12,14},{14,12},{16,18},{18,... | collective-permute-start | bytes 442376 | tf_op jit(solution)/shard_map/ppermute | solution.py:272
  19.4 0.7 %collective-permute-start.9 = (bf16[576,128]{1,0:T(8,128)(2,1)S(1)}, bf16[576,128]{1,0:T(8,128)(2,1)S(1)}, u32[]{:S(2)}, u32[]{:S(2)}) collective-permute-start(bf16[576,128]{1,0:T(8,128)(2,1)S(1)} %finish_keys.1.refs_0_), channel_id=1, source_target_pairs={{0,24},{2,26},{4,28},{6,30},{1,25},{3,27},{5,29},{7,31}} | collective-permute-start | bytes 442376 | tf_op jit(solution)/shard_map/ppermute | solution.py:276
  20.1 0.0 collective-permute-done.13.refs_1_
  20.1 0.1 collective-permute-start.15
  20.2 0.0 collective-permute-done.1.refs_0_
  20.2 3.1 %collective-permute-start.5 = (bf16[576,128]{1,0:T(8,128)(2,1)S(1)}, bf16[576,128]{1,0:T(8,128)(2,1)S(1)}, u32[]{:S(2)}, u32[]{:S(2)}) collective-permute-start(bf16[576,128]{1,0:T(8,128)(2,1)S(1)} %collective-permute-done.1.refs_0_), channel_id=1, source_target_pairs={{0,8},{2,10},{4,12},{6,14},{8,16},{10,18},{12,20},{14,22},{16,24},... | collective-permute-start | bytes 442376 | tf_op jit(solution)/shard_map/ppermute | solution.py:276
  23.3 0.9 %collective-permute-start.3 = (bf16[576,128]{1,0:T(8,128)(2,1)S(1)}, bf16[576,128]{1,0:T(8,128)(2,1)S(1)}, u32[]{:S(2)}, u32[]{:S(2)}) collective-permute-start(bf16[576,128]{1,0:T(8,128)(2,1)S(1)} %collective-permute-done.1.refs_0_), channel_id=1, source_target_pairs={{0,4},{2,6},{4,0},{6,2},{8,12},{10,14},{12,8},{14,10},{16,20},{18,... | collective-permute-start | bytes 442376 | tf_op jit(solution)/shard_map/ppermute | solution.py:272
  24.2 0.0 collective-permute-done.14.refs_2_
  24.2 3.0 %collective-permute-start.2 = (bf16[576,128]{1,0:T(8,128)(2,1)S(1)}, bf16[576,128]{1,0:T(8,128)(2,1)S(1)}, u32[]{:S(2)}, u32[]{:S(2)}) collective-permute-start(bf16[576,128]{1,0:T(8,128)(2,1)S(1)} %collective-permute-done.1.refs_0_), channel_id=1, source_target_pairs={{0,2},{2,0},{4,6},{6,4},{8,10},{10,8},{12,14},{14,12},{16,18},{18,... | collective-permute-start | bytes 442376 | tf_op jit(solution)/shard_map/ppermute | solution.py:272
  27.2 0.0 collective-permute-done.9.refs_3_
  27.2 1.2 %collective-permute-start.10 = (bf16[576,128]{1,0:T(8,128)(2,1)S(1)}, bf16[576,128]{1,0:T(8,128)(2,1)S(1)}, u32[]{:S(2)}, u32[]{:S(2)}) collective-permute-start(bf16[576,128]{1,0:T(8,128)(2,1)S(1)} %collective-permute-done.9.refs_3_), channel_id=1, source_target_pairs={{0,4},{2,6},{4,0},{6,2},{8,12},{10,14},{12,8},{14,10},{16,20},{18,... | collective-permute-start | bytes 442376 | tf_op jit(solution)/shard_map/ppermute | solution.py:272
  28.4 0.0 collective-permute-done.15.refs_3_
  28.4 0.3 collective-permute-start.11
  28.7 0.3 collective-permute-done.5.refs_2_
  29.0 0.2 collective-permute-start.6
  29.2 6.7 %attend.3 = (f32[32,128,512]{2,1,0:T(8,128)S(1)}, f32[32,128,128]{2,1,0:T(8,128)S(1)}, f32[32,128,128]{2,1,0:T(8,128)S(1)}) custom-call(s32[1]{0:T(128)} %bitcast.index_ref, bf16[32,128,512]{2,1,0:T(8,128)(2,1)S(1)} %bitcast.6, bf16[32,128,64]{2,1,0:T(8,128)(2,1)S(1)} %rotate_queries.1.rope_ref, bf16[576,128]{1,0:T(8,128)(2,1)S(1)} %finish_keys.1.refs_0_, ...), custom_call_target="tpu_custom_call" | custom-call | flops 4563402752 | bytes 4718592 | tf_op jit(solution)/shard_map/attend/pallas_call | solution.py:247
  36.0 0.0 collective-permute-done.3.refs_1_
  36.0 1.8 %collective-permute-start.7 = (bf16[576,128]{1,0:T(8,128)(2,1)S(1)}, bf16[576,128]{1,0:T(8,128)(2,1)S(1)}, u32[]{:S(2)}, u32[]{:S(2)}) collective-permute-start(bf16[576,128]{1,0:T(8,128)(2,1)S(1)} %collective-permute-done.5.refs_2_), channel_id=1, source_target_pairs={{0,2},{2,0},{4,6},{6,4},{8,10},{10,8},{12,14},{14,12},{16,18},{18,... | collective-permute-start | bytes 442376 | tf_op jit(solution)/shard_map/ppermute | solution.py:272
  37.8 0.0 collective-permute-done.10.refs_5_
  37.8 0.1 collective-permute-start.4
  37.9 0.0 collective-permute-done.2.refs_0_
  37.9 0.4 collective-permute-start.12
  38.3 0.0 collective-permute-done.6.refs_2_
  38.3 0.1 collective-permute-start.8
  38.4 0.0 copy-start.2
  38.4 8.2 %attend.4 = (f32[32,128,512]{2,1,0:T(8,128)S(1)}, f32[32,128,128]{2,1,0:T(8,128)S(1)}, f32[32,128,128]{2,1,0:T(8,128)S(1)}) custom-call(s32[1]{0:T(128)} %bitcast.index_ref, bf16[32,128,512]{2,1,0:T(8,128)(2,1)S(1)} %bitcast.7, bf16[32,128,64]{2,1,0:T(8,128)(2,1)S(1)} %rotate_queries.1.rope_ref, ...), custom_call_target="tpu_custom_call", output_to_operand_aliasing={{0}: (7, {}), {1}: (8, {}), {2}: (9, {})} | custom-call | flops 4563402752 | bytes 4718592 | tf_op jit(solution)/shard_map/attend/pallas_call | solution.py:247
  46.6 0.0 collective-permute-done.11.refs_6_
  46.6 0.0 collective-permute-done.7.refs_3_
  46.6 0.0 collective-permute-done.4.refs_1_
  46.6 0.0 collective-permute-done.12.refs_7_
  46.6 0.0 collective-permute-done.8.refs_4_
  46.6 0.0 copy-done.2
  46.6 16.0 %attend.5 = bf16[128,4096]{1,0:T(8,128)(2,1)} custom-call(s32[1]{0:T(128)} %bitcast.index_ref, bf16[32,128,512]{2,1,0:T(8,128)(2,1)S(1)} %bitcast.8, bf16[32,128,64]{2,1,0:T(8,128)(2,1)S(1)} %rotate_queries.1.rope_ref, bf16[576,128]{1,0:T(8,128)(2,1)S(1)} %collective-permute-done.2.refs_0_, bf16[576,128]{1,0:T(8,128)(2,1)S(1)} %collective-permute-done.4.refs_1_, ...), custom_call_target="tpu_custom_call" | custom-call | flops 9126805504 | bytes 4718592 | tf_op jit(solution)/shard_map/attend/pallas_call | solution.py:247
  (3 shorter events, 0.0 us)
Async XLA Ops:
  4.3 8.2 %collective-permute-start = (f32[576,128]{1,0:T(8,128)}, f32[576,128]{1,0:T(8,128)S(1)}, u32[]{:S(2)}, u32[]{:S(2)}) collective-permute-start(f32[576,128]{1,0:T(8,128)} %down_project.1.own_ref), channel_id=1, source_target_pairs={{0,1},{1,0},{2,3},{3,2},{4,5},{5,4},{6,7},{7,6},{8,9},{9,8},{10,11... | collective-permute-start | bytes 884744 | tf_op jit(solution)/shard_map/ppermute | solution.py:281
  4.7 5.1 %copy-start.1 = (bf16[128,2048]{1,0:T(8,128)(2,1)S(1)}, bf16[128,2048]{1,0:T(8,128)(2,1)}, u32[]{:S(2)}) copy-start(bf16[128,2048]{1,0:T(8,128)(2,1)} %query_ref.1) | copy-start | bytes 1572868
  4.7 7.8 %copy-start.3 = (f32[512]{0:T(512)S(1)}, f32[512]{0:T(512)}, u32[]{:S(2)}) copy-start(f32[512]{0:T(512)} %param.8) | copy-start | bytes 6148
  4.7 8.0 %copy-start = (f32[576,128]{1,0:T(8,128)S(1)}, f32[576,128]{1,0:T(8,128)}, u32[]{:S(2)}) copy-start(f32[576,128]{1,0:T(8,128)} %down_project.1.own_ref) | copy-start | bytes 884740
  12.8 7.3 %collective-permute-start.13 = (bf16[576,128]{1,0:T(8,128)(2,1)S(1)}, bf16[576,128]{1,0:T(8,128)(2,1)S(1)}, u32[]{:S(2)}, u32[]{:S(2)}) collective-permute-start(bf16[576,128]{1,0:T(8,128)(2,1)S(1)} %finish_keys.1.refs_0_), channel_id=1, source_target_pairs={{0,4},{2,6},{4,0},{6,2},{8,12},{10,14},{12,8},{14,10},{16,20},{18,... | collective-permute-start | bytes 442376 | tf_op jit(solution)/shard_map/ppermute | solution.py:272
  14.1 6.1 %collective-permute-start.1 = (bf16[576,128]{1,0:T(8,128)(2,1)S(1)}, bf16[576,128]{1,0:T(8,128)(2,1)S(1)}, u32[]{:S(2)}, u32[]{:S(2)}) collective-permute-start(bf16[576,128]{1,0:T(8,128)(2,1)S(1)} %finish_keys.1.refs_0_), channel_id=1, source_target_pairs={{0,8},{2,10},{4,12},{6,14},{8,16},{10,18},{12,20},{14,22},{16,24},... | collective-permute-start | bytes 442376 | tf_op jit(solution)/shard_map/ppermute | solution.py:276
  17.3 6.9 %collective-permute-start.14 = (bf16[576,128]{1,0:T(8,128)(2,1)S(1)}, bf16[576,128]{1,0:T(8,128)(2,1)S(1)}, u32[]{:S(2)}, u32[]{:S(2)}) collective-permute-start(bf16[576,128]{1,0:T(8,128)(2,1)S(1)} %finish_keys.1.refs_0_), channel_id=1, source_target_pairs={{0,2},{2,0},{4,6},{6,4},{8,10},{10,8},{12,14},{14,12},{16,18},{18,... | collective-permute-start | bytes 442376 | tf_op jit(solution)/shard_map/ppermute | solution.py:272
  19.4 7.7 %collective-permute-start.9 = (bf16[576,128]{1,0:T(8,128)(2,1)S(1)}, bf16[576,128]{1,0:T(8,128)(2,1)S(1)}, u32[]{:S(2)}, u32[]{:S(2)}) collective-permute-start(bf16[576,128]{1,0:T(8,128)(2,1)S(1)} %finish_keys.1.refs_0_), channel_id=1, source_target_pairs={{0,24},{2,26},{4,28},{6,30},{1,25},{3,27},{5,29},{7,31}} | collective-permute-start | bytes 442376 | tf_op jit(solution)/shard_map/ppermute | solution.py:276
  20.1 8.3 %collective-permute-start.15 = (bf16[576,128]{1,0:T(8,128)(2,1)S(1)}, bf16[576,128]{1,0:T(8,128)(2,1)S(1)}, u32[]{:S(2)}, u32[]{:S(2)}) collective-permute-start(bf16[576,128]{1,0:T(8,128)(2,1)S(1)} %collective-permute-done.13.refs_1_), channel_id=1, source_target_pairs={{0,2},{2,0},{4,6},{6,4},{8,10},{10,8},{12,14},{14,12},{16,18},{18,... | collective-permute-start | bytes 442376 | tf_op jit(solution)/shard_map/ppermute | solution.py:272
  20.2 8.8 %collective-permute-start.5 = (bf16[576,128]{1,0:T(8,128)(2,1)S(1)}, bf16[576,128]{1,0:T(8,128)(2,1)S(1)}, u32[]{:S(2)}, u32[]{:S(2)}) collective-permute-start(bf16[576,128]{1,0:T(8,128)(2,1)S(1)} %collective-permute-done.1.refs_0_), channel_id=1, source_target_pairs={{0,8},{2,10},{4,12},{6,14},{8,16},{10,18},{12,20},{14,22},{16,24},... | collective-permute-start | bytes 442376 | tf_op jit(solution)/shard_map/ppermute | solution.py:276
  23.3 12.6 %collective-permute-start.3 = (bf16[576,128]{1,0:T(8,128)(2,1)S(1)}, bf16[576,128]{1,0:T(8,128)(2,1)S(1)}, u32[]{:S(2)}, u32[]{:S(2)}) collective-permute-start(bf16[576,128]{1,0:T(8,128)(2,1)S(1)} %collective-permute-done.1.refs_0_), channel_id=1, source_target_pairs={{0,4},{2,6},{4,0},{6,2},{8,12},{10,14},{12,8},{14,10},{16,20},{18,... | collective-permute-start | bytes 442376 | tf_op jit(solution)/shard_map/ppermute | solution.py:272
  24.2 13.7 %collective-permute-start.2 = (bf16[576,128]{1,0:T(8,128)(2,1)S(1)}, bf16[576,128]{1,0:T(8,128)(2,1)S(1)}, u32[]{:S(2)}, u32[]{:S(2)}) collective-permute-start(bf16[576,128]{1,0:T(8,128)(2,1)S(1)} %collective-permute-done.1.refs_0_), channel_id=1, source_target_pairs={{0,2},{2,0},{4,6},{6,4},{8,10},{10,8},{12,14},{14,12},{16,18},{18,... | collective-permute-start | bytes 442376 | tf_op jit(solution)/shard_map/ppermute | solution.py:272
  27.2 10.6 %collective-permute-start.10 = (bf16[576,128]{1,0:T(8,128)(2,1)S(1)}, bf16[576,128]{1,0:T(8,128)(2,1)S(1)}, u32[]{:S(2)}, u32[]{:S(2)}) collective-permute-start(bf16[576,128]{1,0:T(8,128)(2,1)S(1)} %collective-permute-done.9.refs_3_), channel_id=1, source_target_pairs={{0,4},{2,6},{4,0},{6,2},{8,12},{10,14},{12,8},{14,10},{16,20},{18,... | collective-permute-start | bytes 442376 | tf_op jit(solution)/shard_map/ppermute | solution.py:272
  28.4 18.2 %collective-permute-start.11 = (bf16[576,128]{1,0:T(8,128)(2,1)S(1)}, bf16[576,128]{1,0:T(8,128)(2,1)S(1)}, u32[]{:S(2)}, u32[]{:S(2)}) collective-permute-start(bf16[576,128]{1,0:T(8,128)(2,1)S(1)} %collective-permute-done.9.refs_3_), channel_id=1, source_target_pairs={{0,2},{2,0},{4,6},{6,4},{8,10},{10,8},{12,14},{14,12},{16,18},{18,... | collective-permute-start | bytes 442376 | tf_op jit(solution)/shard_map/ppermute | solution.py:272
  29.0 9.3 %collective-permute-start.6 = (bf16[576,128]{1,0:T(8,128)(2,1)S(1)}, bf16[576,128]{1,0:T(8,128)(2,1)S(1)}, u32[]{:S(2)}, u32[]{:S(2)}) collective-permute-start(bf16[576,128]{1,0:T(8,128)(2,1)S(1)} %collective-permute-done.5.refs_2_), channel_id=1, source_target_pairs={{0,4},{2,6},{4,0},{6,2},{8,12},{10,14},{12,8},{14,10},{16,20},{18,... | collective-permute-start | bytes 442376 | tf_op jit(solution)/shard_map/ppermute | solution.py:272
  36.0 10.6 %collective-permute-start.7 = (bf16[576,128]{1,0:T(8,128)(2,1)S(1)}, bf16[576,128]{1,0:T(8,128)(2,1)S(1)}, u32[]{:S(2)}, u32[]{:S(2)}) collective-permute-start(bf16[576,128]{1,0:T(8,128)(2,1)S(1)} %collective-permute-done.5.refs_2_), channel_id=1, source_target_pairs={{0,2},{2,0},{4,6},{6,4},{8,10},{10,8},{12,14},{14,12},{16,18},{18,... | collective-permute-start | bytes 442376 | tf_op jit(solution)/shard_map/ppermute | solution.py:272
  37.8 8.8 %collective-permute-start.4 = (bf16[576,128]{1,0:T(8,128)(2,1)S(1)}, bf16[576,128]{1,0:T(8,128)(2,1)S(1)}, u32[]{:S(2)}, u32[]{:S(2)}) collective-permute-start(bf16[576,128]{1,0:T(8,128)(2,1)S(1)} %collective-permute-done.3.refs_1_), channel_id=1, source_target_pairs={{0,2},{2,0},{4,6},{6,4},{8,10},{10,8},{12,14},{14,12},{16,18},{18,... | collective-permute-start | bytes 442376 | tf_op jit(solution)/shard_map/ppermute | solution.py:272
  37.9 8.7 %collective-permute-start.12 = (bf16[576,128]{1,0:T(8,128)(2,1)S(1)}, bf16[576,128]{1,0:T(8,128)(2,1)S(1)}, u32[]{:S(2)}, u32[]{:S(2)}) collective-permute-start(bf16[576,128]{1,0:T(8,128)(2,1)S(1)} %collective-permute-done.10.refs_5_), channel_id=1, source_target_pairs={{0,2},{2,0},{4,6},{6,4},{8,10},{10,8},{12,14},{14,12},{16,18},{18,... | collective-permute-start | bytes 442376 | tf_op jit(solution)/shard_map/ppermute | solution.py:272
  38.3 8.3 %collective-permute-start.8 = (bf16[576,128]{1,0:T(8,128)(2,1)S(1)}, bf16[576,128]{1,0:T(8,128)(2,1)S(1)}, u32[]{:S(2)}, u32[]{:S(2)}) collective-permute-start(bf16[576,128]{1,0:T(8,128)(2,1)S(1)} %collective-permute-done.6.refs_2_), channel_id=1, source_target_pairs={{0,2},{2,0},{4,6},{6,4},{8,10},{10,8},{12,14},{14,12},{16,18},{18,... | collective-permute-start | bytes 442376 | tf_op jit(solution)/shard_map/ppermute | solution.py:272
  38.4 8.2 %copy-start.2 = (bf16[32,512,128]{2,1,0:T(8,128)(2,1)S(1)}, bf16[32,512,128]{2,1,0:T(8,128)(2,1)}, u32[]{:S(2)}) copy-start(bf16[32,512,128]{2,1,0:T(8,128)(2,1)} %refs_11_.1) | copy-start | bytes 12582916

commit v2 on v1

--- a/solution.py
+++ b/solution.py
@@ -153,7 +153,7 @@
     index = index_ref[0]
     state_refs = [] if first else rest[:3]
     rest = rest[len(state_refs) :]
-    groups = [range(b, min(b + CHUNK, len(tags))) for b in range(0, len(tags), CHUNK)]
+    cut = lambda count: [range(b, min(b + CHUNK, count)) for b in range(0, count, CHUNK)]
     wide = lambda column: jnp.broadcast_to(column, (rows, LANES))
     spread = lambda value, width: jnp.concatenate([value] * (width // LANES), -1)
 
@@ -209,16 +209,18 @@
                 ref[...] = value.reshape(ref.shape)
 
     if first:
-        run(groups)
+        run(cut(len(tags)))
         return
-    lowest = [min(tags[i][1] for i in group) for group in groups]
-    needed = sum((index // GROUP >= level).astype(jnp.int32) for level in lowest)
-    cases = sorted({0, 1, len(groups)})
-    for below, case in zip([-1] + cases, cases):
-
-        @pl.when((needed > below) & (needed <= case))
+    levels = sorted({level for _, level in tags})
+    bounds = [0] + (levels if len(levels) <= 3 else levels[:2] + levels[-1:])
+    plane = index // GROUP
+    for below, bound in zip([-1] + bounds, bounds):
+        count = sum(level <= bound for _, level in tags)
+        inside = plane > below if bound == levels[-1] else (plane > below) & (plane <= bound)
+
+        @pl.when(inside)
         def _():
-            run(groups[:case])
+            run(cut(count))
 
 
 def attend(index, latent, rope, tagged, state=(), w_value=None):

time: 62.8 us -> 63 us (level)
  the two profiles are of different devices: /device:TPU:19 before, /device:TPU:31 now
where the time goes in v2:
time: 63 us; the launch traced here: 62.8 us
  Pallas kernels  37.1 us (59%)
  starting transfers between devices  18.7 us (30%)
  local copies, waits for them, and re-layouts  4.75 us (8%)
  waiting for transfers between devices  1.44 us (2%)
  other arithmetic  0.63 us (1%)
    pallas_call x3, Pallas kernels, attend(): pl.pallas_call(functools.partial(attend_kernel, tags, first, last), out_s...  31.2 us
    ppermute x12, starting transfers between devices, from_seq(): return lax.ppermute(value, 'seq', [(i, i ^ xor) for i in range(seq_size)])  14.3 us
    unnamed x9, local copies, waits for them, and re-layouts  4.62 us
    pallas_call x1, Pallas kernels, down_project(): pl.pallas_call(project_kernel, out_shape=jax.ShapeDtypeStruct((width, row...  4.33 us
    ppermute x3, starting transfers between devices, from_below(): lax.ppermute(value, 'seq', [(i, i + shift) for i in range(seq_size - shif...  4.02 us
    pallas_call x1, Pallas kernels, rotate(): pl.pallas_call(rotate_kernel, out_shape=jax.ShapeDtypeStruct((heads, quer...  1.48 us
  transfers between devices with their start and end apart: 16, of which 2 were waited for; matrix products, arithmetic and copies ran while one was open for 8% of the time, Pallas kernels for 26%

profile of v2, /device:TPU:31, one launch (start us, length us, event | category | flops | bytes accessed | tf_op | source)
XLA Modules:
  0.0 62.8 jit_solution(14520716530076659579)
XLA Ops:
  0.0 4.3 %down_project.1.own_ref = f32[576,128]{1,0:T(8,128)} custom-call(bf16[128,3584]{1,0:T(8,128)(2,1)} %hidden_ref.1, bf16[576,3584]{1,0:T(8,128)(2,1)} %bitcast.9), custom_call_target="tpu_custom_call" | custom-call | flops 528482304 | bytes 5046272 | tf_op jit(solution)/shard_map/down_project/pallas_call | solution.py:77
  4.3 0.3 collective-permute-start
  4.7 0.0 copy-start.1
  4.7 0.0 copy-start.3
  4.7 0.0 copy-start
  4.7 4.6 %copy.14 = bf16[128,32,512]{2,0,1:T(8,128)(2,1)S(1)} copy(bf16[128,32,512]{2,1,0:T(8,128)(2,1)} %param.9) | data formatting | bytes 8388608 | tf_op args[3]
  9.3 0.3 fusion
  9.6 0.2 pad_maximum_fusion
  9.8 0.0 copy-done.1
  9.8 1.5 %rotate_queries.1.rope_ref = bf16[32,128,64]{2,1,0:T(8,128)(2,1)S(1)} custom-call(bf16[128,2048]{1,0:T(8,128)(2,1)S(1)} %copy-done.1, f32[128,128]{1,0:T(8,128)S(1)} %get-tuple-element.22.cos_ref, f32[128,128]{1,0:T(8,128)S(1)} %get-tuple-element.23.sin_ref), custom_call_target="tpu_custom_call" | custom-call | tf_op jit(solution)/shard_map/rotate_queries/pallas_call | solution.py:132
  11.3 0.1 multiply_sine_fusion.1
  11.4 1.1 %collective-permute-done.other_ref = f32[576,128]{1,0:T(8,128)S(1)} collective-permute-done((f32[576,128]{1,0:T(8,128)}, f32[576,128]{1,0:T(8,128)S(1)}, u32[]{:S(2)}, u32[]{:S(2)}) %collective-permute-start) | collective-permute-done | bytes 294944 | tf_op jit(solution)/shard_map/ppermute | solution.py:283
  12.5 0.0 copy-done.3
  12.5 0.1 broadcast_in_dim.2.gain_ref
  12.6 0.0 copy-done
  12.7 0.1 finish_keys.1.refs_0_
  12.8 0.3 collective-permute-start.13
  13.1 1.3 %collective-permute-start.1 = (bf16[576,128]{1,0:T(8,128)(2,1)S(1)}, bf16[576,128]{1,0:T(8,128)(2,1)S(1)}, u32[]{:S(2)}, u32[]{:S(2)}) collective-permute-start(bf16[576,128]{1,0:T(8,128)(2,1)S(1)} %finish_keys.1.refs_0_), channel_id=1, source_target_pairs={{0,8},{2,10},{4,12},{6,14},{8,16},{10,18},{12,20},{14,22},{16,24},... | collective-permute-start | bytes 442376 | tf_op jit(solution)/shard_map/ppermute | solution.py:278
  14.4 1.9 %collective-permute-start.14 = (bf16[576,128]{1,0:T(8,128)(2,1)S(1)}, bf16[576,128]{1,0:T(8,128)(2,1)S(1)}, u32[]{:S(2)}, u32[]{:S(2)}) collective-permute-start(bf16[576,128]{1,0:T(8,128)(2,1)S(1)} %finish_keys.1.refs_0_), channel_id=1, source_target_pairs={{0,2},{2,0},{4,6},{6,4},{8,10},{10,8},{12,14},{14,12},{16,18},{18,... | collective-permute-start | bytes 442376 | tf_op jit(solution)/shard_map/ppermute | solution.py:274
  16.2 1.3 %collective-permute-start.9 = (bf16[576,128]{1,0:T(8,128)(2,1)S(1)}, bf16[576,128]{1,0:T(8,128)(2,1)S(1)}, u32[]{:S(2)}, u32[]{:S(2)}) collective-permute-start(bf16[576,128]{1,0:T(8,128)(2,1)S(1)} %finish_keys.1.refs_0_), channel_id=1, source_target_pairs={{0,24},{2,26},{4,28},{6,30},{1,25},{3,27},{5,29},{7,31}} | collective-permute-start | bytes 442376 | tf_op jit(solution)/shard_map/ppermute | solution.py:278
  17.5 0.0 collective-permute-done.13.refs_1_
  17.5 2.0 %collective-permute-start.15 = (bf16[576,128]{1,0:T(8,128)(2,1)S(1)}, bf16[576,128]{1,0:T(8,128)(2,1)S(1)}, u32[]{:S(2)}, u32[]{:S(2)}) collective-permute-start(bf16[576,128]{1,0:T(8,128)(2,1)S(1)} %collective-permute-done.13.refs_1_), channel_id=1, source_target_pairs={{0,2},{2,0},{4,6},{6,4},{8,10},{10,8},{12,14},{14,12},{16,18},{18,... | collective-permute-start | bytes 442376 | tf_op jit(solution)/shard_map/ppermute | solution.py:274
  19.5 0.0 collective-permute-done.1.refs_0_
  19.5 1.5 %collective-permute-start.5 = (bf16[576,128]{1,0:T(8,128)(2,1)S(1)}, bf16[576,128]{1,0:T(8,128)(2,1)S(1)}, u32[]{:S(2)}, u32[]{:S(2)}) collective-permute-start(bf16[576,128]{1,0:T(8,128)(2,1)S(1)} %collective-permute-done.1.refs_0_), channel_id=1, source_target_pairs={{0,8},{2,10},{4,12},{6,14},{8,16},{10,18},{12,20},{14,22},{16,24},... | collective-permute-start | bytes 442376 | tf_op jit(solution)/shard_map/ppermute | solution.py:278
  21.0 0.7 %collective-permute-start.3 = (bf16[576,128]{1,0:T(8,128)(2,1)S(1)}, bf16[576,128]{1,0:T(8,128)(2,1)S(1)}, u32[]{:S(2)}, u32[]{:S(2)}) collective-permute-start(bf16[576,128]{1,0:T(8,128)(2,1)S(1)} %collective-permute-done.1.refs_0_), channel_id=1, source_target_pairs={{0,4},{2,6},{4,0},{6,2},{8,12},{10,14},{12,8},{14,10},{16,20},{18,... | collective-permute-start | bytes 442376 | tf_op jit(solution)/shard_map/ppermute | solution.py:274
  21.7 0.0 collective-permute-done.14.refs_2_
  21.7 3.2 %collective-permute-start.2 = (bf16[576,128]{1,0:T(8,128)(2,1)S(1)}, bf16[576,128]{1,0:T(8,128)(2,1)S(1)}, u32[]{:S(2)}, u32[]{:S(2)}) collective-permute-start(bf16[576,128]{1,0:T(8,128)(2,1)S(1)} %collective-permute-done.1.refs_0_), channel_id=1, source_target_pairs={{0,2},{2,0},{4,6},{6,4},{8,10},{10,8},{12,14},{14,12},{16,18},{18,... | collective-permute-start | bytes 442376 | tf_op jit(solution)/shard_map/ppermute | solution.py:274
  25.0 0.3 collective-permute-done.9.refs_3_
  25.3 1.2 %collective-permute-start.10 = (bf16[576,128]{1,0:T(8,128)(2,1)S(1)}, bf16[576,128]{1,0:T(8,128)(2,1)S(1)}, u32[]{:S(2)}, u32[]{:S(2)}) collective-permute-start(bf16[576,128]{1,0:T(8,128)(2,1)S(1)} %collective-permute-done.9.refs_3_), channel_id=1, source_target_pairs={{0,4},{2,6},{4,0},{6,2},{8,12},{10,14},{12,8},{14,10},{16,20},{18,... | collective-permute-start | bytes 442376 | tf_op jit(solution)/shard_map/ppermute | solution.py:274
  26.5 0.0 collective-permute-done.15.refs_3_
  26.5 1.6 %collective-permute-start.11 = (bf16[576,128]{1,0:T(8,128)(2,1)S(1)}, bf16[576,128]{1,0:T(8,128)(2,1)S(1)}, u32[]{:S(2)}, u32[]{:S(2)}) collective-permute-start(bf16[576,128]{1,0:T(8,128)(2,1)S(1)} %collective-permute-done.9.refs_3_), channel_id=1, source_target_pairs={{0,2},{2,0},{4,6},{6,4},{8,10},{10,8},{12,14},{14,12},{16,18},{18,... | collective-permute-start | bytes 442376 | tf_op jit(solution)/shard_map/ppermute | solution.py:274
  28.2 0.0 collective-permute-done.5.refs_2_
  28.2 0.8 %collective-permute-start.6 = (bf16[576,128]{1,0:T(8,128)(2,1)S(1)}, bf16[576,128]{1,0:T(8,128)(2,1)S(1)}, u32[]{:S(2)}, u32[]{:S(2)}) collective-permute-start(bf16[576,128]{1,0:T(8,128)(2,1)S(1)} %collective-permute-done.5.refs_2_), channel_id=1, source_target_pairs={{0,4},{2,6},{4,0},{6,2},{8,12},{10,14},{12,8},{14,10},{16,20},{18,... | collective-permute-start | bytes 442376 | tf_op jit(solution)/shard_map/ppermute | solution.py:274
  29.0 6.7 %attend.3 = (f32[32,128,512]{2,1,0:T(8,128)S(1)}, f32[32,128,128]{2,1,0:T(8,128)S(1)}, f32[32,128,128]{2,1,0:T(8,128)S(1)}) custom-call(s32[1]{0:T(128)} %bitcast.index_ref, bf16[32,128,512]{2,1,0:T(8,128)(2,1)S(1)} %bitcast.6, bf16[32,128,64]{2,1,0:T(8,128)(2,1)S(1)} %rotate_queries.1.rope_ref, bf16[576,128]{1,0:T(8,128)(2,1)S(1)} %finish_keys.1.refs_0_, ...), custom_call_target="tpu_custom_call" | custom-call | flops 4563402752 | bytes 4718592 | tf_op jit(solution)/shard_map/attend/pallas_call | solution.py:249
  35.7 0.0 collective-permute-done.3.refs_1_
  35.7 1.9 %collective-permute-start.7 = (bf16[576,128]{1,0:T(8,128)(2,1)S(1)}, bf16[576,128]{1,0:T(8,128)(2,1)S(1)}, u32[]{:S(2)}, u32[]{:S(2)}) collective-permute-start(bf16[576,128]{1,0:T(8,128)(2,1)S(1)} %collective-permute-done.5.refs_2_), channel_id=1, source_target_pairs={{0,2},{2,0},{4,6},{6,4},{8,10},{10,8},{12,14},{14,12},{16,18},{18,... | collective-permute-start | bytes 442376 | tf_op jit(solution)/shard_map/ppermute | solution.py:274
  37.6 0.0 collective-permute-done.10.refs_5_
  37.7 0.1 collective-permute-start.4
  37.7 0.0 collective-permute-done.2.refs_0_
  37.7 0.4 collective-permute-start.12
  38.2 0.0 collective-permute-done.6.refs_2_
  38.2 0.1 collective-permute-start.8
  38.3 0.0 copy-start.2
  38.3 8.2 %attend.4 = (f32[32,128,512]{2,1,0:T(8,128)S(1)}, f32[32,128,128]{2,1,0:T(8,128)S(1)}, f32[32,128,128]{2,1,0:T(8,128)S(1)}) custom-call(s32[1]{0:T(128)} %bitcast.index_ref, bf16[32,128,512]{2,1,0:T(8,128)(2,1)S(1)} %bitcast.7, bf16[32,128,64]{2,1,0:T(8,128)(2,1)S(1)} %rotate_queries.1.rope_ref, ...), custom_call_target="tpu_custom_call", output_to_operand_aliasing={{0}: (7, {}), {1}: (8, {}), {2}: (9, {})} | custom-call | flops 4563402752 | bytes 4718592 | tf_op jit(solution)/shard_map/attend/pallas_call | solution.py:249
  46.5 0.0 collective-permute-done.11.refs_6_
  46.5 0.0 collective-permute-done.7.refs_3_
  46.5 0.0 collective-permute-done.4.refs_1_
  46.5 0.0 collective-permute-done.12.refs_7_
  46.5 0.0 collective-permute-done.8.refs_4_
  46.5 0.0 copy-done.2
  46.5 16.2 %attend.5 = bf16[128,4096]{1,0:T(8,128)(2,1)} custom-call(s32[1]{0:T(128)} %bitcast.index_ref, bf16[32,128,512]{2,1,0:T(8,128)(2,1)S(1)} %bitcast.8, bf16[32,128,64]{2,1,0:T(8,128)(2,1)S(1)} %rotate_queries.1.rope_ref, bf16[576,128]{1,0:T(8,128)(2,1)S(1)} %collective-permute-done.2.refs_0_, bf16[576,128]{1,0:T(8,128)(2,1)S(1)} %collective-permute-done.4.refs_1_, ...), custom_call_target="tpu_custom_call" | custom-call | flops 9126805504 | bytes 4718592 | tf_op jit(solution)/shard_map/attend/pallas_call | solution.py:249
  (3 shorter events, 0.0 us)
Async XLA Ops:
  4.3 8.2 %collective-permute-start = (f32[576,128]{1,0:T(8,128)}, f32[576,128]{1,0:T(8,128)S(1)}, u32[]{:S(2)}, u32[]{:S(2)}) collective-permute-start(f32[576,128]{1,0:T(8,128)} %down_project.1.own_ref), channel_id=1, source_target_pairs={{0,1},{1,0},{2,3},{3,2},{4,5},{5,4},{6,7},{7,6},{8,9},{9,8},{10,11... | collective-permute-start | bytes 884744 | tf_op jit(solution)/shard_map/ppermute | solution.py:283
  4.7 5.1 %copy-start.1 = (bf16[128,2048]{1,0:T(8,128)(2,1)S(1)}, bf16[128,2048]{1,0:T(8,128)(2,1)}, u32[]{:S(2)}) copy-start(bf16[128,2048]{1,0:T(8,128)(2,1)} %query_ref.1) | copy-start | bytes 1572868
  4.7 7.8 %copy-start.3 = (f32[512]{0:T(512)S(1)}, f32[512]{0:T(512)}, u32[]{:S(2)}) copy-start(f32[512]{0:T(512)} %param.8) | copy-start | bytes 6148
  4.7 8.0 %copy-start = (f32[576,128]{1,0:T(8,128)S(1)}, f32[576,128]{1,0:T(8,128)}, u32[]{:S(2)}) copy-start(f32[576,128]{1,0:T(8,128)} %down_project.1.own_ref) | copy-start | bytes 884740
  12.8 4.8 %collective-permute-start.13 = (bf16[576,128]{1,0:T(8,128)(2,1)S(1)}, bf16[576,128]{1,0:T(8,128)(2,1)S(1)}, u32[]{:S(2)}, u32[]{:S(2)}) collective-permute-start(bf16[576,128]{1,0:T(8,128)(2,1)S(1)} %finish_keys.1.refs_0_), channel_id=1, source_target_pairs={{0,4},{2,6},{4,0},{6,2},{8,12},{10,14},{12,8},{14,10},{16,20},{18,... | collective-permute-start | bytes 442376 | tf_op jit(solution)/shard_map/ppermute | solution.py:274
  13.1 6.4 %collective-permute-start.1 = (bf16[576,128]{1,0:T(8,128)(2,1)S(1)}, bf16[576,128]{1,0:T(8,128)(2,1)S(1)}, u32[]{:S(2)}, u32[]{:S(2)}) collective-permute-start(bf16[576,128]{1,0:T(8,128)(2,1)S(1)} %finish_keys.1.refs_0_), channel_id=1, source_target_pairs={{0,8},{2,10},{4,12},{6,14},{8,16},{10,18},{12,20},{14,22},{16,24},... | collective-permute-start | bytes 442376 | tf_op jit(solution)/shard_map/ppermute | solution.py:278
  14.4 7.4 %collective-permute-start.14 = (bf16[576,128]{1,0:T(8,128)(2,1)S(1)}, bf16[576,128]{1,0:T(8,128)(2,1)S(1)}, u32[]{:S(2)}, u32[]{:S(2)}) collective-permute-start(bf16[576,128]{1,0:T(8,128)(2,1)S(1)} %finish_keys.1.refs_0_), channel_id=1, source_target_pairs={{0,2},{2,0},{4,6},{6,4},{8,10},{10,8},{12,14},{14,12},{16,18},{18,... | collective-permute-start | bytes 442376 | tf_op jit(solution)/shard_map/ppermute | solution.py:274
  16.2 9.1 %collective-permute-start.9 = (bf16[576,128]{1,0:T(8,128)(2,1)S(1)}, bf16[576,128]{1,0:T(8,128)(2,1)S(1)}, u32[]{:S(2)}, u32[]{:S(2)}) collective-permute-start(bf16[576,128]{1,0:T(8,128)(2,1)S(1)} %finish_keys.1.refs_0_), channel_id=1, source_target_pairs={{0,24},{2,26},{4,28},{6,30},{1,25},{3,27},{5,29},{7,31}} | collective-permute-start | bytes 442376 | tf_op jit(solution)/shard_map/ppermute | solution.py:278
  17.5 9.0 %collective-permute-start.15 = (bf16[576,128]{1,0:T(8,128)(2,1)S(1)}, bf16[576,128]{1,0:T(8,128)(2,1)S(1)}, u32[]{:S(2)}, u32[]{:S(2)}) collective-permute-start(bf16[576,128]{1,0:T(8,128)(2,1)S(1)} %collective-permute-done.13.refs_1_), channel_id=1, source_target_pairs={{0,2},{2,0},{4,6},{6,4},{8,10},{10,8},{12,14},{14,12},{16,18},{18,... | collective-permute-start | bytes 442376 | tf_op jit(solution)/shard_map/ppermute | solution.py:274
  19.5 8.7 %collective-permute-start.5 = (bf16[576,128]{1,0:T(8,128)(2,1)S(1)}, bf16[576,128]{1,0:T(8,128)(2,1)S(1)}, u32[]{:S(2)}, u32[]{:S(2)}) collective-permute-start(bf16[576,128]{1,0:T(8,128)(2,1)S(1)} %collective-permute-done.1.refs_0_), channel_id=1, source_target_pairs={{0,8},{2,10},{4,12},{6,14},{8,16},{10,18},{12,20},{14,22},{16,24},... | collective-permute-start | bytes 442376 | tf_op jit(solution)/shard_map/ppermute | solution.py:278
  21.0 14.7 %collective-permute-start.3 = (bf16[576,128]{1,0:T(8,128)(2,1)S(1)}, bf16[576,128]{1,0:T(8,128)(2,1)S(1)}, u32[]{:S(2)}, u32[]{:S(2)}) collective-permute-start(bf16[576,128]{1,0:T(8,128)(2,1)S(1)} %collective-permute-done.1.refs_0_), channel_id=1, source_target_pairs={{0,4},{2,6},{4,0},{6,2},{8,12},{10,14},{12,8},{14,10},{16,20},{18,... | collective-permute-start | bytes 442376 | tf_op jit(solution)/shard_map/ppermute | solution.py:274
  21.7 16.0 %collective-permute-start.2 = (bf16[576,128]{1,0:T(8,128)(2,1)S(1)}, bf16[576,128]{1,0:T(8,128)(2,1)S(1)}, u32[]{:S(2)}, u32[]{:S(2)}) collective-permute-start(bf16[576,128]{1,0:T(8,128)(2,1)S(1)} %collective-permute-done.1.refs_0_), channel_id=1, source_target_pairs={{0,2},{2,0},{4,6},{6,4},{8,10},{10,8},{12,14},{14,12},{16,18},{18,... | collective-permute-start | bytes 442376 | tf_op jit(solution)/shard_map/ppermute | solution.py:274
  25.3 12.4 %collective-permute-start.10 = (bf16[576,128]{1,0:T(8,128)(2,1)S(1)}, bf16[576,128]{1,0:T(8,128)(2,1)S(1)}, u32[]{:S(2)}, u32[]{:S(2)}) collective-permute-start(bf16[576,128]{1,0:T(8,128)(2,1)S(1)} %collective-permute-done.9.refs_3_), channel_id=1, source_target_pairs={{0,4},{2,6},{4,0},{6,2},{8,12},{10,14},{12,8},{14,10},{16,20},{18,... | collective-permute-start | bytes 442376 | tf_op jit(solution)/shard_map/ppermute | solution.py:274
  26.5 19.9 %collective-permute-start.11 = (bf16[576,128]{1,0:T(8,128)(2,1)S(1)}, bf16[576,128]{1,0:T(8,128)(2,1)S(1)}, u32[]{:S(2)}, u32[]{:S(2)}) collective-permute-start(bf16[576,128]{1,0:T(8,128)(2,1)S(1)} %collective-permute-done.9.refs_3_), channel_id=1, source_target_pairs={{0,2},{2,0},{4,6},{6,4},{8,10},{10,8},{12,14},{14,12},{16,18},{18,... | collective-permute-start | bytes 442376 | tf_op jit(solution)/shard_map/ppermute | solution.py:274
  28.2 10.0 %collective-permute-start.6 = (bf16[576,128]{1,0:T(8,128)(2,1)S(1)}, bf16[576,128]{1,0:T(8,128)(2,1)S(1)}, u32[]{:S(2)}, u32[]{:S(2)}) collective-permute-start(bf16[576,128]{1,0:T(8,128)(2,1)S(1)} %collective-permute-done.5.refs_2_), channel_id=1, source_target_pairs={{0,4},{2,6},{4,0},{6,2},{8,12},{10,14},{12,8},{14,10},{16,20},{18,... | collective-permute-start | bytes 442376 | tf_op jit(solution)/shard_map/ppermute | solution.py:274
  35.7 10.8 %collective-permute-start.7 = (bf16[576,128]{1,0:T(8,128)(2,1)S(1)}, bf16[576,128]{1,0:T(8,128)(2,1)S(1)}, u32[]{:S(2)}, u32[]{:S(2)}) collective-permute-start(bf16[576,128]{1,0:T(8,128)(2,1)S(1)} %collective-permute-done.5.refs_2_), channel_id=1, source_target_pairs={{0,2},{2,0},{4,6},{6,4},{8,10},{10,8},{12,14},{14,12},{16,18},{18,... | collective-permute-start | bytes 442376 | tf_op jit(solution)/shard_map/ppermute | solution.py:274
  37.7 8.8 %collective-permute-start.4 = (bf16[576,128]{1,0:T(8,128)(2,1)S(1)}, bf16[576,128]{1,0:T(8,128)(2,1)S(1)}, u32[]{:S(2)}, u32[]{:S(2)}) collective-permute-start(bf16[576,128]{1,0:T(8,128)(2,1)S(1)} %collective-permute-done.3.refs_1_), channel_id=1, source_target_pairs={{0,2},{2,0},{4,6},{6,4},{8,10},{10,8},{12,14},{14,12},{16,18},{18,... | collective-permute-start | bytes 442376 | tf_op jit(solution)/shard_map/ppermute | solution.py:274
  37.7 8.8 %collective-permute-start.12 = (bf16[576,128]{1,0:T(8,128)(2,1)S(1)}, bf16[576,128]{1,0:T(8,128)(2,1)S(1)}, u32[]{:S(2)}, u32[]{:S(2)}) collective-permute-start(bf16[576,128]{1,0:T(8,128)(2,1)S(1)} %collective-permute-done.10.refs_5_), channel_id=1, source_target_pairs={{0,2},{2,0},{4,6},{6,4},{8,10},{10,8},{12,14},{14,12},{16,18},{18,... | collective-permute-start | bytes 442376 | tf_op jit(solution)/shard_map/ppermute | solution.py:274
  38.2 8.3 %collective-permute-start.8 = (bf16[576,128]{1,0:T(8,128)(2,1)S(1)}, bf16[576,128]{1,0:T(8,128)(2,1)S(1)}, u32[]{:S(2)}, u32[]{:S(2)}) collective-permute-start(bf16[576,128]{1,0:T(8,128)(2,1)S(1)} %collective-permute-done.6.refs_2_), channel_id=1, source_target_pairs={{0,2},{2,0},{4,6},{6,4},{8,10},{10,8},{12,14},{14,12},{16,18},{18,... | collective-permute-start | bytes 442376 | tf_op jit(solution)/shard_map/ppermute | solution.py:274
  38.3 8.3 %copy-start.2 = (bf16[32,512,128]{2,1,0:T(8,128)(2,1)S(1)}, bf16[32,512,128]{2,1,0:T(8,128)(2,1)}, u32[]{:S(2)}) copy-start(bf16[32,512,128]{2,1,0:T(8,128)(2,1)} %refs_11_.1) | copy-start | bytes 12582916
